TPU v7x, 256 devices: a 8x8x2 block of a 8x8x16 slice. The times are simulated.
256 devices in a mesh: clips: 2 (over z), rows: 128 (over x, y, core).
Axes of the slice: x: 8, y: 8, z: 2, core: 2. Of those that a mesh axis runs over, the one named last changes fastest.
The devices are a block of a 8x8x16 slice.
Arguments:
- tokens: bfloat16 [1024, 120, 2240], P(('clips', 'rows')), parts along dimension 0, may hold values from -16 to 16
- shift: float32 [4480], P('clips'), parts along dimension 0, may hold values from -5 to 5
- scale: float32 [4480], P('clips'), parts along dimension 0, may hold values from -3 to 3
- gate: float32 [4480], P('clips'), parts along dimension 0, may hold values from -5 to 5
- query_weight: bfloat16 [2240, 1280], P(None, 'rows'), may hold values from -0.125 to 0.125
- pair_weight: bfloat16 [2240, 2560], P(None, 'rows'), may hold values from -0.125 to 0.125
- output_weight: bfloat16 [1280, 2240], P('rows'), may hold values from -0.15625 to 0.15625
- depth_taps: float32 [9, 1280], replicated, may hold values from -2 to 2
Outputs:
- block_out: bfloat16 [1024, 120, 2240], P(('clips', 'rows')), parts along dimension 0
- kv_state: float32 [80, 32, 32], P('clips'), parts along dimension 0
There are 2 independent parts, one for each index of `clips`. A program takes and returns all parts, laid end to end along the dimension named above; an argument that names none is the same for every part. Nothing has to cross between parts.
All inputs are finite; a program needn't handle non-finite values.
Results may differ from a plain program's by a relative error of at most 0.0041.
The roundings to bfloat16 on the way count: a program that leaves them out, or rounds other values in their place, can miss the bound.
Values may be sent and summed in bfloat16 or wider, within the bound.
A program may use at most 128 MiB of HBM per device.

v0:
```python
import jax
import jax.numpy as jnp
from jax import lax
from jax.sharding import PartitionSpec as P

HEADS = 40
HEAD = 32
FRAMES = 8
HD = 1280


NORM_EPS = 1e-06
DENOM_EPS = 1e-06


def in_one(arrays, axis):
    vector, at, finished = (jnp.concatenate([a.reshape(-1) for a in arrays]), 0, [])
    running = lax.psum(vector, axis)
    for a in arrays:
        finished.append(running[at : at + a.size].reshape(a.shape))
        at += a.size
    return tuple(finished)


def shifted(shard, axis, by):
    count = lax.axis_size(axis)
    pairs = [(i, i + by) for i in range(count) if 0 <= i + by < count]
    return lax.ppermute(shard, axis, pairs)


def modulate(tokens, shift, scale):
    values = tokens.astype(jnp.float32)
    center = values - jnp.mean(values, axis=-1, keepdims=True)
    spread = jnp.mean(center * center, axis=-1, keepdims=True)
    return (center * lax.rsqrt(spread + NORM_EPS) * (1.0 + scale) + shift).astype(jnp.bfloat16)


def gather_queries(normed, query_weight):
    product = jnp.dot(
        normed,
        lax.all_gather(query_weight, "rows", axis=1, tiled=True),
        preferred_element_type=jnp.float32,
    )
    return jnp.maximum(product, 0.0).astype(jnp.bfloat16)


def gather_pairs(normed, pair_weight):
    return jnp.dot(
        normed,
        lax.all_gather(pair_weight, "rows", axis=1, tiled=True),
        preferred_element_type=jnp.float32,
    )


def state_terms(pair):
    keys = jnp.maximum(pair[:, :HD], 0.0).astype(jnp.bfloat16)
    values = pair[:, HD:].astype(jnp.bfloat16)
    key_heads = keys.reshape(-1, HEADS, HEAD)
    value_heads = values.reshape(-1, HEADS, HEAD)
    state_part = jnp.einsum(
        "thd,the->hde", key_heads, value_heads, preferred_element_type=jnp.float32
    )
    key_part = jnp.sum(key_heads, axis=0, dtype=jnp.float32)
    return (values, state_part, key_part)


def sum_states(state_part, key_part):
    return in_one((state_part, key_part), "rows")


def band_conv(values, depth_taps, band, width):
    grid = values.reshape(band, width, HD)
    above = shifted(grid[band - 1 :], "rows", FRAMES)
    below = shifted(grid[:1], "rows", -FRAMES)
    padded = jnp.concatenate([above, grid, below], axis=0)
    padded = jnp.pad(padded, ((0, 0), (1, 1), (0, 0)))
    result = jnp.zeros((band, width, HD), jnp.float32)
    for step_row in range(3):
        for step_col in range(3):
            taken = padded[step_row : step_row + band, step_col : step_col + width]
            result = result + depth_taps[3 * step_row + step_col] * taken
    return result.reshape(band * width, HD)


def body(tokens, shift, scale, gate, query_weight, pair_weight, output_weight, depth_taps):
    band, width, model = tokens.shape
    normed = modulate(tokens, shift, scale).reshape(band * width, model)
    query = gather_queries(normed, query_weight)
    pair = gather_pairs(normed, pair_weight)
    values, state_part, key_part = state_terms(pair)
    state, key_sum = sum_states(state_part, key_part)
    kv_state = state / (band * width * lax.axis_size("rows"))
    local = band_conv(values, depth_taps, band, width)
    query_heads = query.astype(jnp.float32).reshape(-1, HEADS, HEAD)
    numerator = jnp.einsum("thd,hde->the", query_heads, state, precision=lax.Precision.HIGHEST)
    denominator = (
        jnp.einsum("thd,hd->th", query_heads, key_sum, precision=lax.Precision.HIGHEST) + DENOM_EPS
    )
    linear = (numerator / denominator[:, :, None]).reshape(-1, HD)
    mixed = (linear + local).astype(jnp.bfloat16)
    projected = jnp.dot(
        mixed,
        lax.all_gather(output_weight, "rows", axis=0, tiled=True),
        preferred_element_type=jnp.float32,
    )
    result = tokens.reshape(-1, model).astype(jnp.float32) + gate * projected
    return (result.astype(jnp.bfloat16).reshape(band, width, model), kv_state)


def solution(mesh):
    in_specs = (
        P(("clips", "rows"), None, None),
        P("clips"),
        P("clips"),
        P("clips"),
        P(None, "rows"),
        P(None, "rows"),
        P("rows", None),
        P(),
    )
    out_specs = (P(("clips", "rows"), None, None), P("clips", None, None))
    return jax.shard_map(body, mesh=mesh, in_specs=in_specs, out_specs=out_specs, check_vma=False)
```

profile of v0, /device:TPU:513, one launch (start us, length us, event | category | flops | bytes accessed | tf_op | source)
XLA Modules:
  0.0 567.3 jit_solution(17995378525327666471)
XLA Ops:
  7.2 0.0 copy-start
  7.2 0.1 all-gather.9.cloned.1.call-start
  7.3 0.7 all-gather.9.cloned.1.call-update
  8.0 0.1 all-gather.11.cloned.1.call-start
  8.1 0.7 all-gather.11.cloned.1.call-update
  8.8 0.1 all-gather.7.cloned.1.call-start
  8.9 0.7 all-gather.7.cloned.1.call-update
  9.6 0.1 all-reduce.3.cloned.1.call-start
  9.7 2.0 slice_reduce_fusion.8
  11.6 2.0 convert_reduce_fusion
  13.7 0.7 multiply_reduce_fusion
  14.4 2.2 add_convert_fusion
  16.7 98.1 %all-gather.9.cloned.1.call-done = bf16[128,10,2240]{2,1,0:T(8,128)(2,1)} async-done(((bf16[1,10,2240]{2,1,0:T(8,128)(2,1)}), bf16[128,10,2240]{2,1,0:T(8,128)(2,1)}) %all-gather.9.cloned.1.call-update) | async-done | bytes 5734416 | tf_op jit(solution)/shard_map/all_gather | solution.py:41
  114.7 11.1 %reshape.93 = bf16[1280,2240]{1,0:T(8,128)(2,1)} reshape(bf16[128,10,2240]{2,1,0:T(8,128)(2,1)} %all-gather.9.cloned.1.call-done) | data formatting | bytes 11468800
  125.9 6.5 %fusion.3 = bf16[480,1280]{1,0:T(8,128)(2,1)S(1)} fusion(bf16[480,2240]{1,0:T(8,128)(2,1)} %bitcast.53, bf16[1280,2240]{1,0:T(8,128)(2,1)} %reshape.93), kind=kOutput, calls=%fused_computation.10 | convolution fusion | flops 2753740800 | bytes 9113600 | tf_op jit(solution)/shard_map/dot_general | solution.py:39
  132.3 1.5 copy.23
  133.8 65.8 %all-gather.11.cloned.1.call-done = bf16[128,10,2240]{2,1,0:T(8,128)(2,1)} async-done(((bf16[1,10,2240]{2,1,0:T(8,128)(2,1)}), bf16[128,10,2240]{2,1,0:T(8,128)(2,1)}) %all-gather.11.cloned.1.call-update) | async-done | bytes 5734416 | tf_op jit(solution)/shard_map/all_gather | solution.py:103
  199.6 11.1 %reshape.95 = bf16[1280,2240]{1,0:T(8,128)(2,1)} reshape(bf16[128,10,2240]{2,1,0:T(8,128)(2,1)} %all-gather.11.cloned.1.call-done) | data formatting | bytes 11468800
  210.8 80.1 %all-gather.7.cloned.1.call-done = bf16[128,20,2240]{2,1,0:T(8,128)(2,1)} async-done(((bf16[1,20,2240]{2,1,0:T(8,128)(2,1)}), bf16[128,20,2240]{2,1,0:T(8,128)(2,1)}) %all-gather.7.cloned.1.call-update) | async-done | bytes 11468816 | tf_op jit(solution)/shard_map/all_gather | solution.py:50
  290.8 18.7 %reshape.91 = bf16[2560,2240]{1,0:T(8,128)(2,1)} reshape(bf16[128,20,2240]{2,1,0:T(8,128)(2,1)} %all-gather.7.cloned.1.call-done) | data formatting | bytes 22937600
  309.5 9.5 %fusion.13 = bf16[480,2560]{1,0:T(8,128)(2,1)S(1)} fusion(bf16[480,2240]{1,0:T(8,128)(2,1)} %bitcast.54, bf16[2560,2240]{1,0:T(8,128)(2,1)} %reshape.91), kind=kOutput, calls=%fused_computation.43 | convolution fusion | flops 5505024000 | bytes 16076800 | tf_op jit(solution)/shard_map/dot_general | solution.py:48
  319.0 0.1 slice.118
  319.1 1.6 convert_reduce_fusion.1
  320.7 0.1 copy-done.1
  320.8 2.4 copy.21
  323.2 1.5 copy.22
  324.7 3.0 fusion.14
  327.7 1.9 reshape.81
  329.7 1.6 pad_maximum_fusion.2
  331.3 0.1 all-reduce.3.cloned.1.call-update
  331.3 1.9 slice_bitcast_fusion.1
  333.3 6.8 %collective-permute-start = (bf16[1,120,1280]{2,1,0:T(8,128)(2,1)}, bf16[1,120,1280]{2,1,0:T(8,128)(2,1)}, u32[]{:S(2)}, u32[]{:S(2)}) collective-permute-start(bf16[1,120,1280]{2,1,0:T(8,128)(2,1)} %get-tuple-element.19), channel_id=1, source_target_pairs={{0,8},{1,9},{2,10},{3,11},{4,12},{5,13},{6,14},{7,15},{8,16},{9,17... | collective-permute-start | bytes 921608 | tf_op jit(solution)/shard_map/ppermute | solution.py:28
  340.0 1.5 collective-permute-start.1
  341.5 184.9 %all-reduce.3.cloned.1.call-done = f32[42240]{0:T(1024)} async-done(((f32[42240]{0:T(1024)}), f32[42240]{0:T(1024)}) %all-reduce.3.cloned.1.call-update) | async-done | bytes 168976 | tf_op jit(solution)/shard_map/psum | solution.py:18
  526.4 0.7 slice.120
  527.1 0.1 reshape.96
  527.2 1.9 fusion.15
  529.1 1.6 slice.119
  530.7 2.0 reshape.82
  532.7 2.0 broadcast_multiply_fusion
  534.7 2.2 copy.26
  536.9 4.3 bitcast_divide_fusion
  541.2 0.0 collective-permute-done
  541.2 1.6 fusion.10
  542.9 4.5 multiply_add_fusion
  547.3 3.2 copy.25
  550.6 3.0 fusion.4
  553.6 7.2 %fusion.1 = bf16[480,2240]{1,0:T(8,128)(2,1)} fusion(bf16[480,1280]{0,1:T(8,128)(2,1)S(1)} %fusion.4, bf16[1280,2240]{1,0:T(8,128)(2,1)} %reshape.95, f32[2240]{0:T(1024)S(1)} %copy-done.9, bf16[480,2240]{1,0:T(8,128)(2,1)S(1)} %bitcast.45), kind=kOutput, calls=%fused_computation.6 | convolution fusion | flops 2756812800 | bytes 11272960 | tf_op jit(solution)/shard_map/dot_general | solution.py:101
  (23 shorter events, 0.1 us)
Async XLA Ops:
  7.2 6.5 %copy-start = (bf16[4,120,2240]{2,1,0:T(8,128)(2,1)S(1)}, bf16[4,120,2240]{2,1,0:T(8,128)(2,1)}, u32[]{:S(2)}) copy-start(bf16[4,120,2240]{2,1,0:T(8,128)(2,1)} %param.8) | copy-start | bytes 6451204
  7.2 7.2 %copy-start.8 = (f32[2240]{0:T(1024)S(1)}, f32[2240]{0:T(1024)}, u32[]{:S(2)}) copy-start(f32[2240]{0:T(1024)} %param.10) | copy-start | bytes 26884
  7.2 7.2 %copy-start.7 = (f32[2240]{0:T(1024)S(1)}, f32[2240]{0:T(1024)}, u32[]{:S(2)}) copy-start(f32[2240]{0:T(1024)} %param.9) | copy-start | bytes 26884
  7.2 107.5 %all-gather.9.cloned.1.call-start = ((), (), s32[]{:S(2)}) async-start(), calls=%async_computation.2 | async-start | bytes 9510912 | tf_op jit(solution)/shard_map/all_gather | solution.py:41
  8.0 191.6 %all-gather.11.cloned.1.call-start = ((), (), s32[]{:S(2)}) async-start(), calls=%async_computation.3 | async-start | bytes 9510912 | tf_op jit(solution)/shard_map/all_gather | solution.py:103
  8.8 282.0 %all-gather.7.cloned.1.call-start = ((), (), s32[]{:S(2)}) async-start(), calls=%async_computation.1 | async-start | bytes 14266368 | tf_op jit(solution)/shard_map/all_gather | solution.py:50
  9.6 516.8 %all-reduce.3.cloned.1.call-start = ((), (), s32[]{:S(2)}) async-start(), calls=%async_computation | async-start | bytes 344064 | tf_op jit(solution)/shard_map/psum | solution.py:18
  319.0 1.8 copy-start.1
  333.3 208.0 %collective-permute-start = (bf16[1,120,1280]{2,1,0:T(8,128)(2,1)}, bf16[1,120,1280]{2,1,0:T(8,128)(2,1)}, u32[]{:S(2)}, u32[]{:S(2)}) collective-permute-start(bf16[1,120,1280]{2,1,0:T(8,128)(2,1)} %get-tuple-element.19), channel_id=1, source_target_pairs={{0,8},{1,9},{2,10},{3,11},{4,12},{5,13},{6,14},{7,15},{8,16},{9,17... | collective-permute-start | bytes 921608 | tf_op jit(solution)/shard_map/ppermute | solution.py:28
  340.0 201.2 %collective-permute-start.1 = (bf16[1,120,1280]{2,1,0:T(8,128)(2,1)}, bf16[1,120,1280]{2,1,0:T(8,128)(2,1)}, u32[]{:S(2)}, u32[]{:S(2)}) collective-permute-start(bf16[1,120,1280]{2,1,0:T(8,128)(2,1)} %get-tuple-element.20), channel_id=1, source_target_pairs={{8,0},{9,1},{10,2},{11,3},{12,4},{13,5},{14,6},{15,7},{16,8},{17,9... | collective-permute-start | bytes 921608 | tf_op jit(solution)/shard_map/ppermute | solution.py:28
  541.2 1.6 copy-start.2
  541.2 1.6 copy-start.3
  541.2 1.6 copy-start.4
  541.2 1.7 copy-start.5
  541.2 1.7 copy-start.6
  550.6 3.0 copy-start.9
Sparse Core Ops, SparseCore 0:
  10.6 104.0 all-gather.8
  117.3 82.2 all-gather.10
  202.3 88.4 all-gather.6
  331.5 194.9 all-reduce.2
where the time goes:
time: 569 us; the launch traced here: 567 us
  waiting for transfers between devices  431 us (76%)
  local copies, waits for them, and re-layouts  62.1 us (11%)
  matrix products  32.4 us (6%)
  other arithmetic  19.2 us (3%)
  between operations  14 us (2%)
  starting transfers between devices  8.5 us (1%)
    psum x1, waiting for transfers between devices, in_one(): running = lax.psum(vector, axis)  185 us
    all_gather x1, waiting for transfers between devices, gather_queries(): lax.all_gather(query_weight, 'rows', axis=1, tiled=True)  98.1 us
    all_gather x1, waiting for transfers between devices, gather_pairs(): lax.all_gather(pair_weight, 'rows', axis=1, tiled=True)  80.1 us
    all_gather x1, waiting for transfers between devices, body(): lax.all_gather(output_weight, 'rows', axis=0, tiled=True)  65.8 us
    unnamed x24, local copies, waits for them, and re-layouts  43.3 us
  transfers between devices with their start and end apart: 6, of which 4 were waited for; matrix products, arithmetic and copies ran while one was open for 9% of the time, Pallas kernels for 0%

commit v1 on v0

v1 whole, which is shorter than its diff:
```python
import jax
import jax.numpy as jnp
from jax import lax
from jax.experimental import pallas as pl
from jax.experimental.pallas import tpu as pltpu
from jax.sharding import PartitionSpec as P

HEADS, HEAD, FRAMES, HD = 40, 32, 8, 1280
NORM_EPS = 1e-06
DENOM_EPS = 1e-06
SIDE = 8
UNIT = 80
D = 2240
KP = 2304
WA, WB = 640, 512
BASE1 = 2 * WA
F32, BF16 = jnp.float32, jnp.bfloat16
NT = (((1,), (1,)), ((), ()))
TN = (((0,), (0,)), ((), ()))
NN = (((1,), (0,)), ((), ()))


def mm(lhs, rhs, dims):
    return lax.dot_general(lhs, rhs, dims, preferred_element_type=F32)


def rem(v, m):
    return lax.rem(v + m, m)


def gather_parts(kvsh, qsh, osh, W0, W1, st_kv, st_qo, tmp, p0s, p0r, q0s, q0r, r1s, r1r, r2s, r2r, sbs, sbr):
    r = lax.axis_index("rows")
    c = lax.rem(r, 2)
    y = lax.rem(r // 2, SIDE)
    x = r // (2 * SIDE)
    j, p = y // 2, lax.rem(y, 2)
    i4 = y // 4
    t_me = lax.rem(y // 2, 2)
    a = jnp.where(c == 0, y, x)
    b = jnp.where(c == 0, x, y)
    wid = {0: WA, 1: WB}

    def dev(xx, yy, cc):
        return {"rows": (xx * SIDE + yy) * 2 + cc}

    def at_ring(aa, bb):
        xx = jnp.where(c == 0, bb, aa)
        yy = jnp.where(c == 0, aa, bb)
        return dev(xx, yy, c)

    def by_core(fn):
        for cc in (0, 1):
            @pl.when(c == cc)
            def _(cc=cc):
                fn(cc)

    def coff(cc, pp):
        return pl.multiple_of(pp * WA, 128) if cc == 0 else pl.multiple_of(BASE1 + pp * WB, 128)

    def piece(cc, s, aa, bb):
        xx, yy = (bb, aa) if cc == 0 else (aa, bb)
        cols = pl.ds(coff(cc, lax.rem(yy, 2)), wid[cc])
        if s == 0:
            return W0.at[xx, yy // 2, :, cols]
        return W1.at[lax.rem(yy // 2, 2), xx, yy // 4, :, cols]

    def barrier():
        sem = pltpu.get_barrier_semaphore()
        n = 0
        for m in range(1, 8):
            q = lax.rem(lax.rem(y, 4) * 2 + c + m, 8)
            pl.semaphore_signal(sem, inc=1, device_id=dev(x, 4 * i4 + q // 2, lax.rem(q, 2)))
            pl.semaphore_signal(sem, inc=1, device_id=dev(rem(x + m, SIDE), y, c))
            pl.semaphore_signal(sem, inc=1, device_id=dev(x, rem(y + m, SIDE), c))
            n += 3
        total = 2 * SIDE * SIDE
        for step in (SIDE, total - SIDE):
            pl.semaphore_signal(sem, inc=1, device_id={"rows": lax.rem(r + step, total)})
            n += 1
        pl.semaphore_wait(sem, n)

    def rcopy(src, dst, ss, rs, d):
        return pltpu.make_async_remote_copy(src_ref=src, dst_ref=dst, send_sem=ss, recv_sem=rs, device_id=d,
                                            device_id_type=pl.DeviceIdType.MESH)

    def kv0(m):
        pd, cd = m // 2, m % 2
        src = kvsh.at[:, pl.ds(cd * BASE1 + pd * wid[cd], wid[cd])]
        slot = 2 * p + c
        dst = st_kv.at[slot, :, pl.ds(0, wid[cd])]
        return src, dst, slot, dev(x, 2 * j + pd, cd), (2 * p + c) == m

    def qo0(m):
        yd, cd = m // 2, m % 2
        pd, td = yd % 2, yd // 2
        sh = qsh if td == 0 else osh
        src = sh.at[:, pl.ds(cd * BASE1 + pd * wid[cd], wid[cd])]
        slot = lax.rem(y, 4) * 2 + c
        dst = st_qo.at[slot, :, pl.ds(0, wid[cd])]
        return src, dst, slot, dev(x, 4 * i4 + yd, cd), slot == m

    def phase0_start(n, what, ss, rs):
        for m in range(n):
            src, dst, slot, d, own = what(m)

            @pl.when(own)
            def _():
                pltpu.make_async_copy(src, dst, rs.at[m]).start()

            @pl.when(jnp.logical_not(own))
            def _():
                rcopy(src, dst, ss.at[m], rs.at[slot], d).start()

    def phase0_wait(n, what, stage, ss, rs):
        for m in range(n):
            def w(cc):
                ref = stage.at[m, :, pl.ds(0, wid[cc])]
                pltpu.make_async_copy(ref, ref, rs.at[m]).wait()
            by_core(w)

    def phase0_drain(n, what, ss, rs):
        for m in range(n):
            src, dst, slot, d, own = what(m)

            @pl.when(jnp.logical_not(own))
            def _():
                rcopy(src, dst, ss.at[m], rs.at[slot], d).wait_send()

    def build(s, n, stage):
        rows = UNIT // n
        for m in range(n):
            tmp[m * rows:(m + 1) * rows, :] = stage[m].astype(jnp.float32)

        def put(cc):
            piece(cc, s, a, b)[...] = tmp[:, :wid[cc]].astype(jnp.bfloat16)
        by_core(put)

    def ap(e):
        d = (e + 1) // 2
        return rem(a + jnp.where(lax.rem(e, 2) == 1, -d, d), SIDE), d

    def ring1(s, e, wait_only=False):
        aa, d = ap(e)
        odd = lax.rem(e, 2) == 1

        def cp(cc, dr, aa_):
            ref = piece(cc, s, aa_, b)
            return rcopy(ref, ref, r1s.at[s, dr, aa_], r1r.at[s, aa_], at_ring(rem(a + (1 if dr == 0 else SIDE - 1), SIDE), b))

        @pl.when(e > 0)
        def _():
            by_core(lambda cc: cp(cc, 0, aa).wait_recv())
        right = jnp.logical_or(e == 0, jnp.logical_and(odd, d < 4))
        left = jnp.logical_or(e == 0, jnp.logical_and(jnp.logical_not(odd), d < 3))

        @pl.when(right)
        def _():
            by_core(lambda cc: cp(cc, 0, aa).start())

        @pl.when(left)
        def _():
            by_core(lambda cc: cp(cc, 1, aa).start())

    def ring1_drain(s):
        @pl.loop(0, 8)
        def _(e):
            aa, d = ap(e)
            odd = lax.rem(e, 2) == 1

            def cp(cc, dr):
                ref = piece(cc, s, aa, b)
                return rcopy(ref, ref, r1s.at[s, dr, aa], r1r.at[s, aa], at_ring(rem(a + 1, SIDE), b))

            @pl.when(jnp.logical_or(e == 0, jnp.logical_and(odd, d < 4)))
            def _():
                by_core(lambda cc: cp(cc, 0).wait_send())

            @pl.when(jnp.logical_or(e == 0, jnp.logical_and(jnp.logical_not(odd), d < 3)))
            def _():
                by_core(lambda cc: cp(cc, 1).wait_send())

    def cp2(cc, s, dr, bb, aa, dl, e):
        ref = piece(cc, s, aa, bb)
        return rcopy(ref, ref, r2s.at[s, dr, dl, e], r2r.at[s, bb, aa], at_ring(a, rem(b + (1 if dr == 0 else SIDE - 1), SIDE)))

    def ring2(s, dl, e, wait):
        aa, _ = ap(e)
        for dr in (0, 1):
            bb = rem(b + (-dl if dr == 0 else dl), SIDE)
            if wait:
                by_core(lambda cc: cp2(cc, s, dr, bb, aa, dl, e).wait_recv())
            go = jnp.logical_or(dl < 3, (e < 4) if dr == 0 else (e >= 4))

            @pl.when(go)
            def _():
                by_core(lambda cc: cp2(cc, s, dr, bb, aa, dl, e).start())

    def ring2_last(s, e):
        aa, _ = ap(e)
        bb = rem(b + 4, SIDE)
        by_core(lambda cc: cp2(cc, s, 0, bb, aa, 3, e).wait_recv())

    def ring2_drain(s):
        @pl.loop(0, 32)
        def _(t):
            dl, e = t // 8, lax.rem(t, 8)
            aa, _ = ap(e)
            for dr in (0, 1):
                go = jnp.logical_or(dl < 3, (e < 4) if dr == 0 else (e >= 4))

                @pl.when(go)
                def _():
                    by_core(lambda cc: cp2(cc, s, dr, b, aa, dl, e).wait_send())

    def sib_ref(cc, s, bb):
        if cc == 0:
            cols = pl.ds(0, 2 * WA)
            return W0.at[bb, :, :, cols] if s == 0 else W1.at[:, bb, :, :, cols]
        cols = pl.ds(coff(1, lax.rem(bb, 2)), WB)
        if s == 0:
            return W0.at[:, bb // 2, :, cols]
        return W1.at[lax.rem(bb // 2, 2), :, bb // 4, :, cols]

    def sib(cc, s, bb):
        ref = sib_ref(cc, s, bb)
        return rcopy(ref, ref, sbs.at[s, bb], sbr.at[s, bb], dev(x, y, 1 - c))

    def sib_start(s, bb):
        by_core(lambda cc: sib(cc, s, bb).start())

    def sib_wait(s):
        @pl.loop(0, SIDE)
        def _(bb):
            by_core(lambda cc: sib(1 - cc, s, bb).wait_recv())

    def sib_drain(s):
        @pl.loop(0, SIDE)
        def _(bb):
            by_core(lambda cc: sib(cc, s, bb).wait_send())

    ns = dict(locals())
    return ns


def drain(S):
    S.phase0_drain(4, S.kv0, S.p0s, S.p0r)
    S.phase0_drain(8, S.qo0, S.q0s, S.q0r)
    for s in (0, 1):
        S.ring1_drain(s)
        S.ring2_drain(s)
        S.sib_drain(s)


class Parts:
    pass


def kernel(tok, shift, scale, gate, taps, kvsh, qsh, osh, out, kvs,
           W0, W1, st_kv, st_qo, tmp, p0s, p0r, q0s, q0r, r1s, r1r, r2s, r2r, sbs, sbr,
           normed, keys, vals, vpad, local, mixed, hsend, hrecv, pay, ara, red, rsx, part, agy, tot, fin,
           hs, hr, aas, aar, xs, xr, ys, yr, zs, zr, es, er):
    S = Parts()
    S.__dict__.update(gather_parts(kvsh, qsh, osh, W0, W1, st_kv, st_qo, tmp, p0s, p0r, q0s, q0r, r1s, r1r,
                                   r2s, r2r, sbs, sbr))
    r, x, y, c, b = S.r, S.x, S.y, S.c, S.b
    total = 2 * SIDE * SIDE
    n_tok, width, band = 480, 120, 4
    kv_w = W0.reshape(2 * HD, KP)
    q_w = W1.at[0].reshape(HD, KP)
    o_w = W1.at[1].reshape(HD, KP)

    def norm():
        normed[:, KP - 128:] = jnp.zeros((n_tok, 128), BF16)

        @pl.loop(0, n_tok // 16)
        def _(i):
            rows = pl.ds(pl.multiple_of(i * 16, 16), 16)
            v = tok[rows, :].astype(F32)
            center = v - jnp.mean(v, axis=-1, keepdims=True)
            spread = jnp.mean(center * center, axis=-1, keepdims=True)
            res = center * lax.rsqrt(spread + NORM_EPS) * (1.0 + scale[...]) + shift[...]
            normed[rows, 0:D] = res.astype(BF16)

    def lanes(i, n):
        return pl.ds(pl.multiple_of(i * n, n), n)

    def value_chunk(i):
        res = mm(normed[...], kv_w[pl.ds(pl.multiple_of(HD + i * 256, 256), 256), :], NT).astype(BF16)
        vals[:, lanes(i, 256)] = res
        wide = res.astype(F32)
        vpad[1:1 + band, :, lanes(i, 256)] = wide.reshape(band, width, 256)
        hsend[0, :, lanes(i, 256)] = wide[0:width].astype(BF16)
        hsend[1, :, lanes(i, 256)] = wide[n_tok - width:].astype(BF16)

    def key_chunk(i):
        res = mm(normed[...], kv_w[lanes(i, 256), :], NT)
        keys[:, lanes(i, 256)] = jnp.maximum(res, 0.0).astype(BF16)

    def q_chunk(i):
        res = mm(normed[...], q_w[lanes(i, 256), :], NT)
        keys[:, lanes(i, 256)] = jnp.maximum(res, 0.0).astype(BF16)

    def block_mask():
        i = lax.broadcasted_iota(jnp.int32, (128, 128), 0) // HEAD
        k = lax.broadcasted_iota(jnp.int32, (128, 128), 1) // HEAD
        return i == k

    def state_group(g):
        k = keys[:, lanes(g, 128)]
        s = mm(k, vals[:, lanes(g, 128)], TN)
        s = jnp.where(block_mask(), s, 0.0)
        s = s[0:32] + s[32:64] + s[64:96] + s[96:128]
        half, gg = g // 5, lax.rem(g, 5)
        pay[half, pl.ds(pl.multiple_of(gg * 32, 32), 32), :] = s
        ks = mm(jnp.ones((8, n_tok), BF16), k, NN)
        pay[half, pl.ds(160 + gg, 1), :] = ks[0:1]

    def halo(k):
        to = rem(r + (total - FRAMES if k == 0 else FRAMES), total)
        return S.rcopy(hsend.at[k], hrecv.at[k], hs.at[k], hr.at[k], {"rows": to})

    def sends(k):
        return r >= FRAMES if k == 0 else r < total - FRAMES

    def halo_start():
        for k in (0, 1):
            pl.when(sends(k))(lambda: halo(k).start())

    def halo_finish():
        for k in (0, 1):
            row = band + 1 if k == 0 else 0

            @pl.when(sends(1 - k))
            def _():
                halo(k).wait_recv()
                vpad[row] = hrecv[k].astype(F32)

            @pl.when(jnp.logical_not(sends(1 - k)))
            def _():
                vpad[row] = jnp.zeros((width, HD), F32)

    def conv_group(g):
        ln = lanes(g, 128)
        tp = taps[:, ln]
        col = lax.broadcasted_iota(jnp.int32, (width, 128), 0)
        acc = [None] * band
        for k in range(band + 2):
            v = vpad[k, :, ln]
            before = jnp.where(col == 0, 0.0, pltpu.roll(v, 1, 0))
            after = jnp.where(col == width - 1, 0.0, pltpu.roll(v, width - 1, 0))
            for o in range(band):
                m = k - o
                if 0 <= m <= 2:
                    term = tp[3 * m:3 * m + 1] * before + tp[3 * m + 1:3 * m + 2] * v + tp[3 * m + 2:3 * m + 3] * after
                    acc[o] = term if acc[o] is None else acc[o] + term
        for o in range(band):
            local[o * width:(o + 1) * width, ln] = acc[o]

    def arm():
        return S.rcopy(pay.at[1 - c], ara, aas, aar, S.dev(x, y, 1 - c))

    def ar_x(m):
        xx = rem(x + m, SIDE)
        return S.rcopy(red.at[xx], rsx.at[x], xs.at[xx], xr.at[x], S.dev(xx, y, c)), xx

    def ar_y(m):
        yy = rem(y + m, SIDE)
        return S.rcopy(part, agy.at[y], ys.at[yy], yr.at[y], S.dev(x, yy, c)), yy

    def ar_z(m):
        xx = rem(x + m, SIDE)
        return S.rcopy(tot, fin.at[c, x], zs.at[xx], zr.at[x], S.dev(xx, y, c)), xx

    def arrived(m, buf, sem, me):
        k = rem(me + m, SIDE)
        pltpu.make_async_copy(buf.at[k], buf.at[k], sem.at[k]).wait()

    def sum8(buf):
        acc = buf[0]
        for k in range(1, SIDE):
            acc = acc + buf[k]
        return acc

    def ar_a():
        arm().start()

    def ar_b():
        arm().wait_recv()
        mine = pay[c] + ara[...]
        for k in range(SIDE):
            red[k] = mine[24 * k:24 * k + 24]
        rsx[x] = red[x]
        for m in range(1, SIDE):
            ar_x(m)[0].start()

    def ar_c():
        for m in range(1, SIDE):
            arrived(m, rsx, xr, x)
        res = sum8(rsx)
        part[...] = res
        agy[y] = res
        for m in range(1, SIDE):
            ar_y(m)[0].start()

    def ar_d():
        for m in range(1, SIDE):
            arrived(m, agy, yr, y)
        res = sum8(agy)
        tot[...] = res
        fin[c, x] = res
        for m in range(1, SIDE):
            ar_z(m)[0].start()

    def fin_copy(h):
        return S.rcopy(fin.at[h], fin.at[h], es, er, S.dev(x, y, 1 - c))

    def ar_e():
        for m in range(1, SIDE):
            k = rem(x + m, SIDE)
            pltpu.make_async_copy(tot, tot, zr.at[k]).wait()
        fin_copy(c).start()

    def ar_drain():
        arm().wait_send()
        for m in range(1, SIDE):
            ar_x(m)[0].wait_send()
            ar_y(m)[0].wait_send()
            ar_z(m)[0].wait_send()
        fin_copy(c).wait_send()
        for k in (0, 1):
            pl.when(sends(k))(lambda: halo(k).wait_send())

    def state_of(g):
        half, gg = g // 5, g % 5
        rows = []
        for k in range(4):
            at = 32 * gg + 8 * k
            rows.append(fin[half, at // 24, at % 24:at % 24 + 8])
        return jnp.concatenate(rows, axis=0), fin[half, 6, 16 + gg:17 + gg]

    def linear_group(g):
        s, ks = state_of(g)
        for h in range(4):
            kvs[4 * g + h] = s[:, 32 * h:32 * h + 32] / float(n_tok * total)
        mask = block_mask()
        bd = jnp.where(mask, jnp.concatenate([s] * 4, axis=0), 0.0)
        kd = jnp.where(mask, jnp.transpose(jnp.broadcast_to(ks, (128, 128))), 0.0)
        rhs = jnp.concatenate([bd, kd], axis=1)
        hi = rhs.astype(BF16)
        rest = rhs - hi.astype(F32)
        mid = rest.astype(BF16)
        lo = (rest - mid.astype(F32)).astype(BF16)
        q = keys[:, 128 * g:128 * g + 128]
        res = mm(q, hi, NN) + mm(q, mid, NN) + mm(q, lo, NN)
        lin = res[:, 0:128] / (res[:, 128:256] + DENOM_EPS)
        mixed[:, 128 * g:128 * g + 128] = (lin + local[:, 128 * g:128 * g + 128]).astype(BF16)

    def out_chunk(cols, n):
        w = o_w[:, pl.ds(cols, 256)]
        res = mm(mixed[...], w, NN)
        if n < 256:
            res = res[:, :n]
        ln = pl.ds(cols, n)
        out[:, ln] = (tok[:, ln].astype(F32) + gate[:, ln] * res).astype(BF16)

    S.barrier()
    S.phase0_start(4, S.kv0, p0s, p0r)
    S.phase0_start(8, S.qo0, q0s, q0r)
    pay[0, 160:192, :] = jnp.zeros((32, 128), F32)
    pay[1, 160:192, :] = jnp.zeros((32, 128), F32)
    S.phase0_wait(4, S.kv0, st_kv, p0s, p0r)
    S.build(0, 4, st_kv)
    S.phase0_wait(8, S.qo0, st_qo, q0s, q0r)

    @pl.loop(0, 8)
    def _(e):
        S.ring1(0, e)
        S.ring2(0, 0, e, False)
    S.build(1, 8, st_qo)
    S.sib_start(0, b)
    norm()

    @pl.loop(0, 24)
    def _(t):
        dl, e = 1 + t // 8, lax.rem(t, 8)
        S.ring2(0, dl, e, True)

        @pl.when(dl == 1)
        def _():
            S.ring1(1, e)

        @pl.when(e == 7)
        def _():
            S.sib_start(0, rem(b - dl, SIDE))
            S.sib_start(0, rem(b + dl, SIDE))

    @pl.loop(0, 8)
    def _(e):
        S.ring2(1, 0, e, False)
        S.ring2_last(0, e)
    S.sib_start(0, rem(b + 4, SIDE))
    S.sib_start(1, b)
    S.sib_wait(0)

    @pl.loop(0, 24)
    def _(t):
        dl, e = 1 + t // 8, lax.rem(t, 8)
        S.ring2(1, dl, e, True)

        @pl.when(e == 7)
        def _():
            S.sib_start(1, rem(b - dl, SIDE))
            S.sib_start(1, rem(b + dl, SIDE))

        @pl.when(t < 5)
        def _():
            value_chunk(t)

        pl.when(t == 4)(halo_start)

        @pl.when(jnp.logical_and(t >= 5, t < 10))
        def _():
            key_chunk(t - 5)

        @pl.when(jnp.logical_and(t >= 10, t < 15))
        def _():
            state_group(2 * (t - 10))
            state_group(2 * (t - 10) + 1)

        pl.when(t == 14)(ar_a)
        pl.when(t == 15)(ar_b)
        pl.when(t == 17)(halo_finish)

        @pl.when(jnp.logical_and(t >= 17, t < 22))
        def _():
            conv_group(2 * (t - 17))
            conv_group(2 * (t - 17) + 1)

        pl.when(t == 19)(ar_c)
        pl.when(t == 22)(ar_d)

    @pl.loop(0, 8)
    def _(e):
        S.ring2_last(1, e)
    S.sib_start(1, rem(b + 4, SIDE))
    ar_e()
    S.sib_wait(1)

    @pl.loop(0, 5)
    def _(i):
        q_chunk(i)
    fin_copy(1 - c).wait_recv()
    for g in range(HD // 128):
        linear_group(g)

    @pl.loop(0, 8)
    def _(i):
        out_chunk(pl.multiple_of(i * 256, 256), 256)
    out_chunk(2048, 192)
    ar_drain()
    drain(S)


def body(tokens, shift, scale, gate, query_weight, pair_weight, output_weight, depth_taps):
    band, width, model = tokens.shape
    n = band * width
    pad = ((0, 0), (0, KP - model))
    dma = pltpu.SemaphoreType.DMA
    vm = pltpu.VMEM
    out, kvs = pl.pallas_call(
        kernel,
        out_shape=(jax.ShapeDtypeStruct((n, model), BF16), jax.ShapeDtypeStruct((HEADS, HEAD, HEAD), F32)),
        in_specs=[pl.BlockSpec(memory_space=vm)] * 8,
        out_specs=[pl.BlockSpec(memory_space=vm)] * 2,
        scratch_shapes=[
            vm((SIDE, 4, UNIT, KP), BF16), vm((2, SIDE, 2, UNIT, KP), BF16),
            vm((4, 20, WA), BF16), vm((8, 10, WA), BF16), vm((UNIT, WA), F32),
            dma((4,)), dma((4,)), dma((8,)), dma((8,)),
            dma((2, 2, 8)), dma((2, 8)), dma((2, 2, 4, 8)), dma((2, 8, 8)), dma((2, 8)), dma((2, 8)),
            vm((n, KP), BF16), vm((n, HD), BF16), vm((n, HD), BF16), vm((band + 2, width, HD), F32),
            vm((n, HD), F32), vm((n, HD), BF16), vm((2, width, HD), BF16), vm((2, width, HD), BF16),
            vm((2, 192, 128), F32), vm((192, 128), F32), vm((SIDE, 24, 128), F32), vm((SIDE, 24, 128), F32),
            vm((24, 128), F32), vm((SIDE, 24, 128), F32), vm((24, 128), F32), vm((2, SIDE, 24, 128), F32),
            dma((2,)), dma((2,)), dma, dma, dma((8,)), dma((8,)), dma((8,)), dma((8,)), dma((8,)), dma((8,)), dma, dma,
        ],
        compiler_params=pltpu.CompilerParams(collective_id=0, has_side_effects=True, vmem_limit_bytes=62 << 20),
    )(
        tokens.reshape(n, model), shift[None], scale[None], gate[None], depth_taps,
        jnp.pad(pair_weight.T, pad), jnp.pad(query_weight.T, pad), jnp.pad(output_weight, pad),
    )
    return out.reshape(band, width, model), kvs


def solution(mesh):
    in_specs = (
        P(("clips", "rows"), None, None),
        P("clips"),
        P("clips"),
        P("clips"),
        P(None, "rows"),
        P(None, "rows"),
        P("rows", None),
        P(),
    )
    out_specs = (P(("clips", "rows"), None, None), P("clips", None, None))
    return jax.shard_map(body, mesh=mesh, in_specs=in_specs, out_specs=out_specs, check_vma=False)
```

time: 569 us -> 179 us (0.31)
  waiting for transfers between devices: 431 us -> 0 us
  Pallas kernels: 0 us -> 164 us
  local copies, waits for them, and re-layouts: 62.1 us -> 13.9 us
  matrix products: 32.4 us -> 0 us
  other arithmetic: 19.2 us -> 0 us
  between operations: 14 us -> 0.64 us
  starting transfers between devices: 8.5 us -> 0 us
    all_gather x3 -> x0, waiting for transfers between devices: 244 us -> none  [the longest x1 98.1 us: gather_queries(): lax.all_gather(query_weight, 'rows', axis=1, tiled=True)]
    psum x1 -> x0, waiting for transfers between devices: 185 us -> none  [in_one(): running = lax.psum(vector, axis)]
    pallas_call x0 -> x1, Pallas kernels: none -> 164 us  [body(): pl.pallas_call(kernel, out_shape=(jax.ShapeDtypeStruct((n, model), BF16),...]
    unnamed x24 -> x2, local copies, waits for them, and re-layouts: 43.3 us -> 5.35 us
    dot_general x6 -> x0, matrix products: 32.4 us -> none  [the longest x1 9.51 us: gather_pairs(): jnp.dot(normed, lax.all_gather(pair_weight, 'rows', axis=1, tiled=True),...]
    ppermute x2 -> x0, starting transfers between devices: 8.26 us -> none  [shifted(): return lax.ppermute(shard, axis, pairs)]
    slice x6 -> x0, local copies, waits for them, and re-layouts: 7.72 us -> none  [the longest x2 2.29 us: in_one(): finished.append(running[at:at + a.size].reshape(a.shape))]
    reshape x4 -> x0, local copies, waits for them, and re-layouts: 7.2 us -> none  [the longest x1 3.22 us: band_conv(): return result.reshape(band * width, HD)]
  transfers between devices with their start and end apart: 6 -> 0, of which waited for: 4 -> 0; matrix products, arithmetic and copies ran while one was open for 9% -> 0% of each run, Pallas kernels for 0% -> 0%
where the time goes in v1:
time: 179 us; the launch traced here: 178 us
  Pallas kernels  164 us (92%)
  local copies, waits for them, and re-layouts  13.9 us (8%)
    pallas_call x1, Pallas kernels, body(): pl.pallas_call(kernel, out_shape=(jax.ShapeDtypeStruct((n, model), BF16),...  164 us
    unnamed x2, local copies, waits for them, and re-layouts  5.35 us

profile of v1, /device:TPU:513, one launch (start us, length us, event | category | flops | bytes accessed | tf_op | source)
XLA Modules:
  0.0 178.4 jit_solution(17925888173107347834)
XLA Ops:
  0.6 1.3 broadcast_in_dim.9.shift
  1.9 1.3 broadcast_in_dim.10.scale
  3.3 1.3 broadcast_in_dim.11.gate
  4.6 1.5 pad.12.qsh
  6.1 1.5 pad.13.osh
  7.6 1.6 pad.11.kvsh
  9.2 163.8 %shard_map.95 = (bf16[480,2240]{1,0:T(8,128)(2,1)}, f32[40,32,32]{2,1,0:T(8,128)}) custom-call(bf16[480,2240]{1,0:T(8,128)(2,1)} %bitcast.4, f32[1,2240]{1,0:T(1,128)} %broadcast_in_dim.9.shift, f32[1,2240]{1,0:T(1,128)} %broadcast_in_dim.10.scale, f32[1,2240]{1,0:T(1,128)} %broadcast_in_dim.11.gate, f32[9,1280]{1,0:T(8,128)} %taps.1, ...), custom_call_target="tpu_custom_call" | custom-call | tf_op jit(solution)/shard_map/pallas_call | solution.py:570
  173.0 2.2 %copy.10 = f32[40,32,32]{0,2,1:T(8,128)} copy(f32[40,32,32]{2,1,0:T(8,128)} %get-tuple-element.7) | data formatting | bytes 327680
  175.2 3.1 %copy.12 = bf16[4,120,2240]{2,1,0:T(8,128)(2,1)} copy(bf16[4,120,2240]{2,1,0:T(8,128)(2,1)} %bitcast.5) | data formatting | bytes 4300800

commit v2 on v1

--- a/solution.py
+++ b/solution.py
@@ -12,8 +12,8 @@
 UNIT = 80
 D = 2240
 KP = 2304
-WA, WB = 640, 512
-BASE1 = 2 * WA
+WIDTHS = ((640, 512), (896, 256))
+WMAX = 896
 F32, BF16 = jnp.float32, jnp.bfloat16
 NT = (((1,), (1,)), ((), ()))
 TN = (((0,), (0,)), ((), ()))
@@ -28,17 +28,16 @@
     return lax.rem(v + m, m)
 
 
-def gather_parts(kvsh, qsh, osh, W0, W1, st_kv, st_qo, tmp, p0s, p0r, q0s, q0r, r1s, r1r, r2s, r2r, sbs, sbr):
+def gather_parts(kvsh, qosh, W0, W1, st_kv, st_qo, tmp, p0s, p0r, q0s, q0r, r1s, r1r, r2s, r2r, sbs, sbr):
     r = lax.axis_index("rows")
     c = lax.rem(r, 2)
     y = lax.rem(r // 2, SIDE)
     x = r // (2 * SIDE)
     j, p = y // 2, lax.rem(y, 2)
     i4 = y // 4
-    t_me = lax.rem(y // 2, 2)
     a = jnp.where(c == 0, y, x)
     b = jnp.where(c == 0, x, y)
-    wid = {0: WA, 1: WB}
+    wid = WIDTHS
 
     def dev(xx, yy, cc):
         return {"rows": (xx * SIDE + yy) * 2 + cc}
@@ -54,15 +53,15 @@
             def _(cc=cc):
                 fn(cc)
 
-    def coff(cc, pp):
-        return pl.multiple_of(pp * WA, 128) if cc == 0 else pl.multiple_of(BASE1 + pp * WB, 128)
+    def coff(s, cc, pp):
+        return pl.multiple_of(cc * 2 * wid[s][0] + pp * wid[s][cc], 128)
 
     def piece(cc, s, aa, bb):
         xx, yy = (bb, aa) if cc == 0 else (aa, bb)
-        cols = pl.ds(coff(cc, lax.rem(yy, 2)), wid[cc])
+        cols = pl.ds(coff(s, cc, lax.rem(yy, 2)), wid[s][cc])
         if s == 0:
             return W0.at[xx, yy // 2, :, cols]
-        return W1.at[lax.rem(yy // 2, 2), xx, yy // 4, :, cols]
+        return W1.at[lax.rem(yy // 2 + xx, 2), xx // 2, lax.rem(xx, 2), yy // 4, :, cols]
 
     def barrier():
         sem = pltpu.get_barrier_semaphore()
@@ -73,9 +72,8 @@
             pl.semaphore_signal(sem, inc=1, device_id=dev(rem(x + m, SIDE), y, c))
             pl.semaphore_signal(sem, inc=1, device_id=dev(x, rem(y + m, SIDE), c))
             n += 3
-        total = 2 * SIDE * SIDE
-        for step in (SIDE, total - SIDE):
-            pl.semaphore_signal(sem, inc=1, device_id={"rows": lax.rem(r + step, total)})
+        for k in (1, -1):
+            pl.semaphore_signal(sem, inc=1, device_id=dev(rem(x + k, SIDE), rem(y + 2 * k, SIDE), c))
             n += 1
         pl.semaphore_wait(sem, n)
 
@@ -85,18 +83,19 @@
 
     def kv0(m):
         pd, cd = m // 2, m % 2
-        src = kvsh.at[:, pl.ds(cd * BASE1 + pd * wid[cd], wid[cd])]
+        w = wid[0][cd]
+        src = kvsh.at[:, pl.ds(cd * 2 * wid[0][0] + pd * w, w)]
         slot = 2 * p + c
-        dst = st_kv.at[slot, :, pl.ds(0, wid[cd])]
+        dst = st_kv.at[slot, :, pl.ds(0, w)]
         return src, dst, slot, dev(x, 2 * j + pd, cd), (2 * p + c) == m
 
     def qo0(m):
         yd, cd = m // 2, m % 2
-        pd, td = yd % 2, yd // 2
-        sh = qsh if td == 0 else osh
-        src = sh.at[:, pl.ds(cd * BASE1 + pd * wid[cd], wid[cd])]
+        pd, td = yd % 2, lax.rem(yd // 2 + x, 2)
+        w = wid[1][cd]
+        src = qosh.at[td, :, pl.ds(cd * 2 * wid[1][0] + pd * w, w)]
         slot = lax.rem(y, 4) * 2 + c
-        dst = st_qo.at[slot, :, pl.ds(0, wid[cd])]
+        dst = st_qo.at[slot, :, pl.ds(0, w)]
         return src, dst, slot, dev(x, 4 * i4 + yd, cd), slot == m
 
     def phase0_start(n, what, ss, rs):
@@ -111,10 +110,10 @@
             def _():
                 rcopy(src, dst, ss.at[m], rs.at[slot], d).start()
 
-    def phase0_wait(n, what, stage, ss, rs):
+    def phase0_wait(n, s, stage, rs):
         for m in range(n):
             def w(cc):
-                ref = stage.at[m, :, pl.ds(0, wid[cc])]
+                ref = stage.at[m, :, pl.ds(0, wid[s][cc])]
                 pltpu.make_async_copy(ref, ref, rs.at[m]).wait()
             by_core(w)
 
@@ -129,10 +128,10 @@
     def build(s, n, stage):
         rows = UNIT // n
         for m in range(n):
-            tmp[m * rows:(m + 1) * rows, :] = stage[m].astype(jnp.float32)
+            tmp[m * rows:(m + 1) * rows, 0:stage.shape[-1]] = stage[m].astype(jnp.float32)
 
         def put(cc):
-            piece(cc, s, a, b)[...] = tmp[:, :wid[cc]].astype(jnp.bfloat16)
+            piece(cc, s, a, b)[...] = tmp[:, :wid[s][cc]].astype(jnp.bfloat16)
         by_core(put)
 
     def ap(e):
@@ -195,10 +194,32 @@
             def _():
                 by_core(lambda cc: cp2(cc, s, dr, bb, aa, dl, e).start())
 
+    def pick(typ, e, bb):
+        at_y = lax.rem(e, 2) + 4 * (e // 2) + 2 * lax.rem(typ + bb, 2)
+        at_x = 2 * e + lax.rem(typ + bb // 2, 2)
+        return jnp.where(c == 0, at_y, at_x)
+
+    def ring2q(typ, dl, e, wait):
+        for dr in (0, 1):
+            bb = rem(b + (-dl if dr == 0 else dl), SIDE)
+            aa = pick(typ, e, bb)
+            if wait:
+                by_core(lambda cc: cp2(cc, 1, dr, bb, aa, dl, 4 * typ + e).wait_recv())
+            go = jnp.logical_or(dl < 3, (e < 2) if dr == 0 else (e >= 2))
+
+            @pl.when(go)
+            def _():
+                by_core(lambda cc: cp2(cc, 1, dr, bb, aa, dl, 4 * typ + e).start())
+
     def ring2_last(s, e):
         aa, _ = ap(e)
         bb = rem(b + 4, SIDE)
         by_core(lambda cc: cp2(cc, s, 0, bb, aa, 3, e).wait_recv())
+
+    def ring2q_last(typ, e):
+        bb = rem(b + 4, SIDE)
+        aa = pick(typ, e, bb)
+        by_core(lambda cc: cp2(cc, 1, 0, bb, aa, 3, e).wait_recv())
 
     def ring2_drain(s):
         @pl.loop(0, 32)
@@ -206,20 +227,22 @@
             dl, e = t // 8, lax.rem(t, 8)
             aa, _ = ap(e)
             for dr in (0, 1):
-                go = jnp.logical_or(dl < 3, (e < 4) if dr == 0 else (e >= 4))
+                ee = e if s == 0 else 2 * lax.rem(e, 4)
+                go = jnp.logical_or(dl < 3, (ee < 4) if dr == 0 else (ee >= 4))
 
                 @pl.when(go)
                 def _():
                     by_core(lambda cc: cp2(cc, s, dr, b, aa, dl, e).wait_send())
 
     def sib_ref(cc, s, bb):
+        w = min(s, 1)
         if cc == 0:
-            cols = pl.ds(0, 2 * WA)
-            return W0.at[bb, :, :, cols] if s == 0 else W1.at[:, bb, :, :, cols]
-        cols = pl.ds(coff(1, lax.rem(bb, 2)), WB)
+            cols = pl.ds(0, 2 * wid[w][0])
+            return W0.at[bb, :, :, cols] if s == 0 else W1.at[s - 1, bb // 2, lax.rem(bb, 2), :, :, cols]
+        cols = pl.ds(coff(w, 1, lax.rem(bb, 2)), wid[w][1])
         if s == 0:
             return W0.at[:, bb // 2, :, cols]
-        return W1.at[lax.rem(bb // 2, 2), :, bb // 4, :, cols]
+        return W1.at[s - 1, :, lax.rem(s - 1 + bb // 2, 2), bb // 4, :, cols]
 
     def sib(cc, s, bb):
         ref = sib_ref(cc, s, bb)
@@ -242,25 +265,17 @@
     return ns
 
 
-def drain(S):
-    S.phase0_drain(4, S.kv0, S.p0s, S.p0r)
-    S.phase0_drain(8, S.qo0, S.q0s, S.q0r)
-    for s in (0, 1):
-        S.ring1_drain(s)
-        S.ring2_drain(s)
-        S.sib_drain(s)
-
-
 class Parts:
     pass
 
 
-def kernel(tok, shift, scale, gate, taps, kvsh, qsh, osh, out, kvs,
+def kernel(tok, shift, scale, gate, taps, kvin, qin, oin, out, kvs,
+           mod, kvsh, qosh,
            W0, W1, st_kv, st_qo, tmp, p0s, p0r, q0s, q0r, r1s, r1r, r2s, r2r, sbs, sbr,
-           normed, keys, vals, vpad, local, mixed, hsend, hrecv, pay, ara, red, rsx, part, agy, tot, fin,
-           hs, hr, aas, aar, xs, xr, ys, yr, zs, zr, es, er):
+           normed, keys, vals, vpad, local, mixed, hsend, hrecv, relay, pay, ara, red, rsx, part, agy, tot, fin,
+           hs, hr, vs, vr, aas, aar, xs, xr, ys, yr, zs, zr, es, er):
     S = Parts()
-    S.__dict__.update(gather_parts(kvsh, qsh, osh, W0, W1, st_kv, st_qo, tmp, p0s, p0r, q0s, q0r, r1s, r1r,
+    S.__dict__.update(gather_parts(kvsh, qosh, W0, W1, st_kv, st_qo, tmp, p0s, p0r, q0s, q0r, r1s, r1r,
                                    r2s, r2r, sbs, sbr))
     r, x, y, c, b = S.r, S.x, S.y, S.c, S.b
     total = 2 * SIDE * SIDE
@@ -269,16 +284,14 @@
     q_w = W1.at[0].reshape(HD, KP)
     o_w = W1.at[1].reshape(HD, KP)
 
-    def norm():
-        normed[:, KP - 128:] = jnp.zeros((n_tok, 128), BF16)
-
-        @pl.loop(0, n_tok // 16)
+    def norm(lo, hi):
+        @pl.loop(lo, hi, unroll=2)
         def _(i):
             rows = pl.ds(pl.multiple_of(i * 16, 16), 16)
             v = tok[rows, :].astype(F32)
             center = v - jnp.mean(v, axis=-1, keepdims=True)
             spread = jnp.mean(center * center, axis=-1, keepdims=True)
-            res = center * lax.rsqrt(spread + NORM_EPS) * (1.0 + scale[...]) + shift[...]
+            res = center * lax.rsqrt(spread + NORM_EPS) * (1.0 + mod[1:2, :]) + mod[0:1, :]
             normed[rows, 0:D] = res.astype(BF16)
 
     def lanes(i, n):
@@ -316,23 +329,39 @@
         pay[half, pl.ds(160 + gg, 1), :] = ks[0:1]
 
     def halo(k):
-        to = rem(r + (total - FRAMES if k == 0 else FRAMES), total)
-        return S.rcopy(hsend.at[k], hrecv.at[k], hs.at[k], hr.at[k], {"rows": to})
+        k2 = 2 if k else -2
+        return S.rcopy(hsend.at[k], relay.at[k], hs.at[k], hr.at[k], S.dev(x, rem(y + k2, SIDE), c))
+
+    def hop(k):
+        k2 = 2 if k else -2
+        origin = S.dev(x, rem(y - k2, SIDE), c)["rows"]
+        to = rem(origin + (FRAMES if k else total - FRAMES), total)
+        has = origin < total - FRAMES if k else origin >= FRAMES
+        return S.rcopy(relay.at[k], hrecv.at[k], vs.at[k], vr.at[k], {"rows": to}), has
 
     def sends(k):
-        return r >= FRAMES if k == 0 else r < total - FRAMES
+        return r < total - FRAMES if k else r >= FRAMES
 
     def halo_start():
         for k in (0, 1):
             pl.when(sends(k))(lambda: halo(k).start())
 
+    def halo_relay():
+        for k in (0, 1):
+            cp, has = hop(k)
+
+            @pl.when(has)
+            def _():
+                halo(k).wait_recv()
+                cp.start()
+
     def halo_finish():
         for k in (0, 1):
             row = band + 1 if k == 0 else 0
 
             @pl.when(sends(1 - k))
             def _():
-                halo(k).wait_recv()
+                hop(k)[0].wait_recv()
                 vpad[row] = hrecv[k].astype(F32)
 
             @pl.when(jnp.logical_not(sends(1 - k)))
@@ -429,6 +458,8 @@
         fin_copy(c).wait_send()
         for k in (0, 1):
             pl.when(sends(k))(lambda: halo(k).wait_send())
+            cp, has = hop(k)
+            pl.when(has)(lambda: cp.wait_send())
 
     def state_of(g):
         half, gg = g // 5, g % 5
@@ -461,110 +492,177 @@
         if n < 256:
             res = res[:, :n]
         ln = pl.ds(cols, n)
-        out[:, ln] = (tok[:, ln].astype(F32) + gate[:, ln] * res).astype(BF16)
-
+        out[:, ln] = (tok[:, ln].astype(F32) + mod[2:3, ln] * res).astype(BF16)
+
+    def level(k, m):
+        return jnp.where(k == 0, 0, 2 * k - 1 + m), jnp.logical_and(
+            jnp.logical_and(k >= 0, k <= 4), jnp.logical_or(m == 0, jnp.logical_and(k >= 1, k <= 3)))
+
+    def drain_first():
+        S.phase0_drain(4, S.kv0, p0s, p0r)
+        S.phase0_drain(8, S.qo0, q0s, q0r)
+        S.ring1_drain(0)
+        S.ring1_drain(1)
+        S.ring2_drain(0)
+        S.sib_drain(0)
+
+    mod[0, :] = shift[...]
+    mod[1, :] = scale[...]
+    mod[2, :] = gate[...]
+    kvsh[:, KP - 128:] = jnp.zeros((20, 128), BF16)
+    qosh[:, :, KP - 128:] = jnp.zeros((2, 10, 128), BF16)
+    kvsh[:, 0:D] = kvin[...]
+    qosh[0, :, 0:D] = qin[...]
+    qosh[1, :, 0:D] = oin[...]
     S.barrier()
     S.phase0_start(4, S.kv0, p0s, p0r)
     S.phase0_start(8, S.qo0, q0s, q0r)
     pay[0, 160:192, :] = jnp.zeros((32, 128), F32)
     pay[1, 160:192, :] = jnp.zeros((32, 128), F32)
-    S.phase0_wait(4, S.kv0, st_kv, p0s, p0r)
+    normed[:, KP - 128:] = jnp.zeros((n_tok, 128), BF16)
+    norm(0, 20)
+    S.phase0_wait(4, 0, st_kv, p0r)
     S.build(0, 4, st_kv)
-    S.phase0_wait(8, S.qo0, st_qo, q0s, q0r)
-
-    @pl.loop(0, 8)
+
+    @pl.loop(0, 64)
+    def _(u):
+        diag, dl, m = u // 8, 3 - lax.rem(u // 2, 4), lax.rem(u, 2)
+        e, valid = level(diag - dl, m)
+
+        @pl.when(jnp.logical_and(valid, dl == 0))
+        def _():
+            S.ring1(0, e)
+            S.ring2(0, 0, e, False)
+
+        @pl.when(jnp.logical_and(valid, dl > 0))
+        def _():
+            S.ring2(0, dl, e, True)
+
+        @pl.when(jnp.logical_and(valid, e == 7))
+        def _():
+            S.sib_start(0, rem(b - dl, SIDE))
+
+            @pl.when(dl > 0)
+            def _():
+                S.sib_start(0, rem(b + dl, SIDE))
+
+        @pl.when(u == 1)
+        def _():
+            norm(20, 24)
+
+        @pl.when(u == 9)
+        def _():
+            norm(24, 30)
+
+        @pl.when(u == 17)
+        def _():
+            S.phase0_wait(8, 1, st_qo, q0r)
+            S.build(1, 8, st_qo)
+
+        step = diag - 3
+        for m2 in (0, 1):
+            e2, ok = level(step, jnp.int32(m2))
+
+            @pl.when(jnp.logical_and(ok, lax.rem(u, 8) == 0))
+            def _():
+                S.ring1(1, e2)
+
+    @pl.loop(0, 4)
     def _(e):
-        S.ring1(0, e)
-        S.ring2(0, 0, e, False)
-    S.build(1, 8, st_qo)
-    S.sib_start(0, b)
-    norm()
-
-    @pl.loop(0, 24)
-    def _(t):
-        dl, e = 1 + t // 8, lax.rem(t, 8)
-        S.ring2(0, dl, e, True)
-
-        @pl.when(dl == 1)
-        def _():
-            S.ring1(1, e)
-
-        @pl.when(e == 7)
-        def _():
-            S.sib_start(0, rem(b - dl, SIDE))
-            S.sib_start(0, rem(b + dl, SIDE))
-
-    @pl.loop(0, 8)
-    def _(e):
-        S.ring2(1, 0, e, False)
+        S.ring2q(0, 0, e, False)
         S.ring2_last(0, e)
+        S.ring2_last(0, e + 4)
     S.sib_start(0, rem(b + 4, SIDE))
     S.sib_start(1, b)
+    S.sib_start(2, b)
     S.sib_wait(0)
 
     @pl.loop(0, 24)
-    def _(t):
-        dl, e = 1 + t // 8, lax.rem(t, 8)
-        S.ring2(1, dl, e, True)
-
-        @pl.when(e == 7)
-        def _():
-            S.sib_start(1, rem(b - dl, SIDE))
-            S.sib_start(1, rem(b + dl, SIDE))
-
-        @pl.when(t < 5)
-        def _():
-            value_chunk(t)
-
-        pl.when(t == 4)(halo_start)
-
-        @pl.when(jnp.logical_and(t >= 5, t < 10))
-        def _():
-            key_chunk(t - 5)
-
-        @pl.when(jnp.logical_and(t >= 10, t < 15))
-        def _():
-            state_group(2 * (t - 10))
-            state_group(2 * (t - 10) + 1)
-
-        pl.when(t == 14)(ar_a)
-        pl.when(t == 15)(ar_b)
-        pl.when(t == 17)(halo_finish)
-
-        @pl.when(jnp.logical_and(t >= 17, t < 22))
-        def _():
-            conv_group(2 * (t - 17))
-            conv_group(2 * (t - 17) + 1)
-
-        pl.when(t == 19)(ar_c)
-        pl.when(t == 22)(ar_d)
-
-    @pl.loop(0, 8)
+    def _(u):
+        typ, dl, e = u // 12, 1 + lax.rem(u // 4, 3), lax.rem(u, 4)
+
+        @pl.when(u == 12)
+        def _():
+            @pl.loop(0, 4)
+            def _(k):
+                S.ring2q(1, 0, k, False)
+        S.ring2q(typ, dl, e, True)
+
+        for ty in (0, 1):
+            @pl.when(jnp.logical_and(e == 3, typ == ty))
+            def _():
+                S.sib_start(1 + ty, rem(b - dl, SIDE))
+                S.sib_start(1 + ty, rem(b + dl, SIDE))
+
+        @pl.when(jnp.logical_and(u >= 12, u < 16))
+        def _():
+            S.ring2q_last(0, e)
+
+        @pl.when(u == 15)
+        def _():
+            S.sib_start(1, rem(b + 4, SIDE))
+
+        @pl.when(u < 5)
+        def _():
+            value_chunk(u)
+
+        pl.when(u == 4)(halo_start)
+
+        @pl.when(jnp.logical_and(u >= 5, u < 10))
+        def _():
+            key_chunk(u - 5)
+
+        @pl.when(jnp.logical_and(u >= 10, u < 12))
+        def _():
+            @pl.loop(0, 5)
+            def _(k):
+                state_group(5 * (u - 10) + k)
+
+        pl.when(u == 10)(halo_relay)
+        pl.when(u == 11)(ar_a)
+        pl.when(u == 12)(ar_b)
+        pl.when(u == 15)(ar_c)
+        pl.when(u == 18)(ar_d)
+        pl.when(u == 17)(drain_first)
+
+        @pl.when(u == 19)
+        def _():
+            S.sib_wait(1)
+
+        @pl.when(u >= 19)
+        def _():
+            q_chunk(u - 19)
+
+        pl.when(u == 21)(ar_e)
+
+    halo_finish()
+
+    @pl.loop(0, 10)
+    def _(g):
+        conv_group(g)
+
+    @pl.loop(0, 4)
     def _(e):
-        S.ring2_last(1, e)
-    S.sib_start(1, rem(b + 4, SIDE))
-    ar_e()
-    S.sib_wait(1)
-
-    @pl.loop(0, 5)
-    def _(i):
-        q_chunk(i)
+        S.ring2q_last(1, e)
+    S.sib_start(2, rem(b + 4, SIDE))
     fin_copy(1 - c).wait_recv()
     for g in range(HD // 128):
         linear_group(g)
+    S.sib_wait(2)
 
     @pl.loop(0, 8)
     def _(i):
         out_chunk(pl.multiple_of(i * 256, 256), 256)
     out_chunk(2048, 192)
     ar_drain()
-    drain(S)
+    S.ring2_drain(1)
+    S.sib_drain(1)
+    S.sib_drain(2)
 
 
 def body(tokens, shift, scale, gate, query_weight, pair_weight, output_weight, depth_taps):
     band, width, model = tokens.shape
     n = band * width
-    pad = ((0, 0), (0, KP - model))
     dma = pltpu.SemaphoreType.DMA
     vm = pltpu.VMEM
     out, kvs = pl.pallas_call(
@@ -573,20 +671,21 @@
         in_specs=[pl.BlockSpec(memory_space=vm)] * 8,
         out_specs=[pl.BlockSpec(memory_space=vm)] * 2,
         scratch_shapes=[
-            vm((SIDE, 4, UNIT, KP), BF16), vm((2, SIDE, 2, UNIT, KP), BF16),
-            vm((4, 20, WA), BF16), vm((8, 10, WA), BF16), vm((UNIT, WA), F32),
+            vm((3, model), F32), vm((20, KP), BF16), vm((2, 10, KP), BF16),
+            vm((SIDE, 4, UNIT, KP), BF16), vm((2, SIDE // 2, 2, 2, UNIT, KP), BF16),
+            vm((4, 20, WIDTHS[0][0]), BF16), vm((8, 10, WMAX), BF16), vm((UNIT, WMAX), F32),
             dma((4,)), dma((4,)), dma((8,)), dma((8,)),
-            dma((2, 2, 8)), dma((2, 8)), dma((2, 2, 4, 8)), dma((2, 8, 8)), dma((2, 8)), dma((2, 8)),
+            dma((2, 2, 8)), dma((2, 8)), dma((2, 2, 4, 8)), dma((2, 8, 8)), dma((3, 8)), dma((3, 8)),
             vm((n, KP), BF16), vm((n, HD), BF16), vm((n, HD), BF16), vm((band + 2, width, HD), F32),
-            vm((n, HD), F32), vm((n, HD), BF16), vm((2, width, HD), BF16), vm((2, width, HD), BF16),
+            vm((n, HD), F32), vm((n, HD), BF16), vm((2, width, HD), BF16), vm((2, width, HD), BF16), vm((2, width, HD), BF16),
             vm((2, 192, 128), F32), vm((192, 128), F32), vm((SIDE, 24, 128), F32), vm((SIDE, 24, 128), F32),
             vm((24, 128), F32), vm((SIDE, 24, 128), F32), vm((24, 128), F32), vm((2, SIDE, 24, 128), F32),
-            dma((2,)), dma((2,)), dma, dma, dma((8,)), dma((8,)), dma((8,)), dma((8,)), dma((8,)), dma((8,)), dma, dma,
+            dma((2,)), dma((2,)), dma((2,)), dma((2,)), dma, dma, dma((8,)), dma((8,)), dma((8,)), dma((8,)), dma((8,)), dma((8,)), dma, dma,
         ],
         compiler_params=pltpu.CompilerParams(collective_id=0, has_side_effects=True, vmem_limit_bytes=62 << 20),
     )(
-        tokens.reshape(n, model), shift[None], scale[None], gate[None], depth_taps,
-        jnp.pad(pair_weight.T, pad), jnp.pad(query_weight.T, pad), jnp.pad(output_weight, pad),
+        tokens.reshape(n, model), shift, scale, gate, depth_taps,
+        pair_weight.T, query_weight.T, output_weight,
     )
     return out.reshape(band, width, model), kvs
 

time: 179 us -> 162 us (0.905)
  local copies, waits for them, and re-layouts: 13.9 us -> 5.35 us
  Pallas kernels: 164 us -> 156 us
    pallas_call x1, Pallas kernels: 164 us -> 156 us  [body(): pl.pallas_call(kernel, out_shape=(jax.ShapeDtypeStruct((n, model), BF16),...]
    pad x3 -> x0, local copies, waits for them, and re-layouts: 4.59 us -> none  [the longest x1 1.55 us: body(): jnp.pad(pair_weight.T, pad)]
    broadcast_in_dim x3 -> x0, local copies, waits for them, and re-layouts: 3.93 us -> none  [the longest x1 1.31 us: body(): scale[None]]
where the time goes in v2:
time: 162 us
  Pallas kernels  156 us (96%)
  local copies, waits for them, and re-layouts  5.35 us (3%)
    pallas_call x1, Pallas kernels, body(): pl.pallas_call(kernel, out_shape=(jax.ShapeDtypeStruct((n, model), BF16),...  156 us
    unnamed x2, local copies, waits for them, and re-layouts  5.35 us

profile of v2, /device:TPU:513, one launch (start us, length us, event | category | flops | bytes accessed | tf_op | source)
XLA Modules:
  0.0 161.8 jit_solution(5896091824340131336)
XLA Ops:
  0.6 155.8 %shard_map.95 = (bf16[480,2240]{1,0:T(8,128)(2,1)}, f32[40,32,32]{2,1,0:T(8,128)}) custom-call(bf16[480,2240]{1,0:T(8,128)(2,1)} %bitcast.4, f32[2240]{0:T(1024)} %shift.1, f32[2240]{0:T(1024)} %scale.1, f32[2240]{0:T(1024)} %gate.1, f32[9,1280]{1,0:T(8,128)} %taps.1, bf16[20,2240]{1,0:T(8,128)(2,1)} %bitcast.6, bf16[10,2240]{1,0:T(8,128)(2,1)} %bitcast.7, ...), custom_call_target="tpu_custom_call" | custom-call | tf_op jit(solution)/shard_map/pallas_call | solution.py:668
  156.4 2.2 %copy.10 = f32[40,32,32]{0,2,1:T(8,128)} copy(f32[40,32,32]{2,1,0:T(8,128)} %get-tuple-element.7) | data formatting | bytes 327680
  158.7 3.1 %copy.12 = bf16[4,120,2240]{2,1,0:T(8,128)(2,1)} copy(bf16[4,120,2240]{2,1,0:T(8,128)(2,1)} %bitcast.5) | data formatting | bytes 4300800

commit v3 on v2

--- a/solution.py
+++ b/solution.py
@@ -28,7 +28,7 @@
     return lax.rem(v + m, m)
 
 
-def gather_parts(kvsh, qosh, W0, W1, st_kv, st_qo, tmp, p0s, p0r, q0s, q0r, r1s, r1r, r2s, r2r, sbs, sbr):
+def gather_parts(kvsh, qosh, W0, W1, st_kv, st_qo, tmp, p0s, p0r, q0s, q0r, r1s, r1r, r2s, r2r, sbs, sbr, pzs):
     r = lax.axis_index("rows")
     c = lax.rem(r, 2)
     y = lax.rem(r // 2, SIDE)
@@ -38,6 +38,9 @@
     a = jnp.where(c == 0, y, x)
     b = jnp.where(c == 0, x, y)
     wid = WIDTHS
+    clip = lax.axis_index("clips")
+    zp = lax.rem(clip, 2)
+    pair = {"clips": clip + 1 - 2 * zp, "rows": r}
 
     def dev(xx, yy, cc):
         return {"rows": (xx * SIDE + yy) * 2 + cc}
@@ -75,7 +78,8 @@
         for k in (1, -1):
             pl.semaphore_signal(sem, inc=1, device_id=dev(rem(x + k, SIDE), rem(y + 2 * k, SIDE), c))
             n += 1
-        pl.semaphore_wait(sem, n)
+        pl.semaphore_signal(sem, inc=1, device_id=pair)
+        pl.semaphore_wait(sem, n + 1)
 
     def rcopy(src, dst, ss, rs, d):
         return pltpu.make_async_remote_copy(src_ref=src, dst_ref=dst, send_sem=ss, recv_sem=rs, device_id=d,
@@ -138,101 +142,130 @@
         d = (e + 1) // 2
         return rem(a + jnp.where(lax.rem(e, 2) == 1, -d, d), SIDE), d
 
-    def ring1(s, e, wait_only=False):
+    def r1copy(cc, s, k, aa, to):
+        ref = piece(cc, s, aa, b)
+        return rcopy(ref, ref, r1s.at[s, k], r1r.at[s, aa], at_ring(rem(a + to, SIDE), b))
+
+    def ring1(s, e):
         aa, d = ap(e)
-        odd = lax.rem(e, 2) == 1
-
-        def cp(cc, dr, aa_):
-            ref = piece(cc, s, aa_, b)
-            return rcopy(ref, ref, r1s.at[s, dr, aa_], r1r.at[s, aa_], at_ring(rem(a + (1 if dr == 0 else SIDE - 1), SIDE), b))
 
         @pl.when(e > 0)
         def _():
-            by_core(lambda cc: cp(cc, 0, aa).wait_recv())
-        right = jnp.logical_or(e == 0, jnp.logical_and(odd, d < 4))
-        left = jnp.logical_or(e == 0, jnp.logical_and(jnp.logical_not(odd), d < 3))
-
-        @pl.when(right)
-        def _():
-            by_core(lambda cc: cp(cc, 0, aa).start())
-
-        @pl.when(left)
-        def _():
-            by_core(lambda cc: cp(cc, 1, aa).start())
+            by_core(lambda cc: r1copy(cc, s, 0, aa, 1).wait_recv())
+
+        if s == 0:
+            plan = ((0, 0, 1), (0, 1, -1), (0, 2, 2), (0, 3, -2), (3, 4, 1), (3, 5, 2), (4, 6, -1))
+        else:
+            plan = ((0, 0, 1), (0, 1, -1), (1, 2, 1), (2, 3, -1), (3, 4, 1), (4, 5, -1), (5, 6, 1))
+        for when, k, to in plan:
+            @pl.when(e == when)
+            def _():
+                by_core(lambda cc: r1copy(cc, s, k, aa, to).start())
 
     def ring1_drain(s):
-        @pl.loop(0, 8)
-        def _(e):
-            aa, d = ap(e)
-            odd = lax.rem(e, 2) == 1
-
-            def cp(cc, dr):
-                ref = piece(cc, s, aa, b)
-                return rcopy(ref, ref, r1s.at[s, dr, aa], r1r.at[s, aa], at_ring(rem(a + 1, SIDE), b))
-
-            @pl.when(jnp.logical_or(e == 0, jnp.logical_and(odd, d < 4)))
-            def _():
-                by_core(lambda cc: cp(cc, 0).wait_send())
-
-            @pl.when(jnp.logical_or(e == 0, jnp.logical_and(jnp.logical_not(odd), d < 3)))
-            def _():
-                by_core(lambda cc: cp(cc, 1).wait_send())
+        @pl.loop(0, 7)
+        def _(k):
+            by_core(lambda cc: r1copy(cc, s, k, a, 1).wait_send())
 
     def cp2(cc, s, dr, bb, aa, dl, e):
         ref = piece(cc, s, aa, bb)
         return rcopy(ref, ref, r2s.at[s, dr, dl, e], r2r.at[s, bb, aa], at_ring(a, rem(b + (1 if dr == 0 else SIDE - 1), SIDE)))
 
-    def ring2(s, dl, e, wait):
-        aa, _ = ap(e)
-        for dr in (0, 1):
-            bb = rem(b + (-dl if dr == 0 else dl), SIDE)
-            if wait:
-                by_core(lambda cc: cp2(cc, s, dr, bb, aa, dl, e).wait_recv())
-            go = jnp.logical_or(dl < 3, (e < 4) if dr == 0 else (e >= 4))
-
-            @pl.when(go)
-            def _():
-                by_core(lambda cc: cp2(cc, s, dr, bb, aa, dl, e).start())
-
-    def pick(typ, e, bb):
+    def by_pair(s, typ, e, plane):
+        if s == 0:
+            return lax.rem(e, 4) == 1 + plane
+        return e == 1 + lax.rem(typ + plane, 2)
+
+    def onward(s, typ, dl, e, dr):
+        low = e < (4 if s == 0 else 2)
+        near = low if dr == 0 else jnp.logical_not(low)
+        return jnp.logical_and(jnp.logical_not(by_pair(s, typ, e, zp)), jnp.logical_or(dl < 3, near))
+
+    def zcopy(cc, s, aa, bb, k, e):
+        ref = piece(cc, s, aa, bb)
+        return rcopy(ref, ref, pzs.at[s, k, e], r2r.at[s, bb, aa], pair)
+
+    def pick(s, typ, e, bb):
+        if s == 0:
+            return ap(e)[0]
         at_y = lax.rem(e, 2) + 4 * (e // 2) + 2 * lax.rem(typ + bb, 2)
         at_x = 2 * e + lax.rem(typ + bb // 2, 2)
         return jnp.where(c == 0, at_y, at_x)
 
-    def ring2q(typ, dl, e, wait):
+    def step2(s, typ, dl, e, wait):
+        e8 = 4 * typ + e
         for dr in (0, 1):
             bb = rem(b + (-dl if dr == 0 else dl), SIDE)
-            aa = pick(typ, e, bb)
+            aa = pick(s, typ, e, bb)
             if wait:
-                by_core(lambda cc: cp2(cc, 1, dr, bb, aa, dl, 4 * typ + e).wait_recv())
-            go = jnp.logical_or(dl < 3, (e < 2) if dr == 0 else (e >= 2))
-
-            @pl.when(go)
-            def _():
-                by_core(lambda cc: cp2(cc, 1, dr, bb, aa, dl, 4 * typ + e).start())
+                @pl.when(jnp.logical_not(by_pair(s, typ, e, zp)))
+                def _():
+                    by_core(lambda cc: cp2(cc, s, dr, bb, aa, dl, e8).wait_recv())
+
+            @pl.when(onward(s, typ, dl, e, dr))
+            def _():
+                by_core(lambda cc: cp2(cc, s, dr, bb, aa, dl, e8).start())
+            if wait:
+                @pl.when(by_pair(s, typ, e, 1 - zp))
+                def _():
+                    by_core(lambda cc: zcopy(cc, s, aa, bb, 2 * dl - 2 + dr, e8).start())
+
+    def last2(s, typ, e):
+        e8 = 4 * typ + e
+        bb = rem(b + 4, SIDE)
+        aa = pick(s, typ, e, bb)
+
+        @pl.when(jnp.logical_not(by_pair(s, typ, e, zp)))
+        def _():
+            by_core(lambda cc: cp2(cc, s, 0, bb, aa, 3, e8).wait_recv())
+
+        @pl.when(by_pair(s, typ, e, 1 - zp))
+        def _():
+            by_core(lambda cc: zcopy(cc, s, aa, bb, 6, e8).start())
+
+    def paired(typ, d):
+        bb = rem(b + d, SIDE)
+        e = 1 + lax.rem(typ + zp, 2)
+        aa = pick(1, typ, e, bb)
+        by_core(lambda cc: cp2(cc, 1, 0, bb, aa, 3, 4 * typ + e).wait_recv())
+
+    def paired0(d):
+        bb = rem(b + d, SIDE)
+        for k in (0, 4):
+            e = k + 1 + zp
+            aa = pick(0, 0, e, bb)
+            by_core(lambda cc: cp2(cc, 0, 0, bb, aa, 3, e).wait_recv())
+
+    def ring2(s, dl, e, wait):
+        step2(0, 0, dl, e, wait)
 
     def ring2_last(s, e):
-        aa, _ = ap(e)
-        bb = rem(b + 4, SIDE)
-        by_core(lambda cc: cp2(cc, s, 0, bb, aa, 3, e).wait_recv())
+        last2(0, 0, e)
+
+    def ring2q(typ, dl, e, wait):
+        step2(1, typ, dl, e, wait)
 
     def ring2q_last(typ, e):
-        bb = rem(b + 4, SIDE)
-        aa = pick(typ, e, bb)
-        by_core(lambda cc: cp2(cc, 1, 0, bb, aa, 3, e).wait_recv())
+        last2(1, typ, e)
 
     def ring2_drain(s):
         @pl.loop(0, 32)
         def _(t):
-            dl, e = t // 8, lax.rem(t, 8)
-            aa, _ = ap(e)
+            dl, e8 = t // 8, lax.rem(t, 8)
+            e, typ = (e8, 0) if s == 0 else (lax.rem(e8, 4), e8 // 4)
             for dr in (0, 1):
-                ee = e if s == 0 else 2 * lax.rem(e, 4)
-                go = jnp.logical_or(dl < 3, (ee < 4) if dr == 0 else (ee >= 4))
-
-                @pl.when(go)
+                @pl.when(onward(s, typ, dl, e, dr))
                 def _():
-                    by_core(lambda cc: cp2(cc, s, dr, b, aa, dl, e).wait_send())
+                    by_core(lambda cc: cp2(cc, s, dr, b, a, dl, e8).wait_send())
+
+        @pl.loop(0, 56)
+        def _(t):
+            k, e8 = t // 8, lax.rem(t, 8)
+            e, typ = (e8, 0) if s == 0 else (lax.rem(e8, 4), e8 // 4)
+
+            @pl.when(by_pair(s, typ, e, 1 - zp))
+            def _():
+                by_core(lambda cc: zcopy(cc, s, a, b, k, e8).wait_send())
 
     def sib_ref(cc, s, bb):
         w = min(s, 1)
@@ -271,13 +304,13 @@
 
 def kernel(tok, shift, scale, gate, taps, kvin, qin, oin, out, kvs,
            mod, kvsh, qosh,
-           W0, W1, st_kv, st_qo, tmp, p0s, p0r, q0s, q0r, r1s, r1r, r2s, r2r, sbs, sbr,
+           W0, W1, st_kv, st_qo, tmp, p0s, p0r, q0s, q0r, r1s, r1r, r2s, r2r, sbs, sbr, pzs,
            normed, keys, vals, vpad, local, mixed, hsend, hrecv, relay, pay, ara, red, rsx, part, agy, tot, fin,
            hs, hr, vs, vr, aas, aar, xs, xr, ys, yr, zs, zr, es, er):
     S = Parts()
     S.__dict__.update(gather_parts(kvsh, qosh, W0, W1, st_kv, st_qo, tmp, p0s, p0r, q0s, q0r, r1s, r1r,
-                                   r2s, r2r, sbs, sbr))
-    r, x, y, c, b = S.r, S.x, S.y, S.c, S.b
+                                   r2s, r2r, sbs, sbr, pzs))
+    r, x, y, c, a, b = S.r, S.x, S.y, S.c, S.a, S.b
     total = 2 * SIDE * SIDE
     n_tok, width, band = 480, 120, 4
     kv_w = W0.reshape(2 * HD, KP)
@@ -328,31 +361,34 @@
         ks = mm(jnp.ones((8, n_tok), BF16), k, NN)
         pay[half, pl.ds(160 + gg, 1), :] = ks[0:1]
 
-    def halo(k):
+    def halo(k, i):
         k2 = 2 if k else -2
-        return S.rcopy(hsend.at[k], relay.at[k], hs.at[k], hr.at[k], S.dev(x, rem(y + k2, SIDE), c))
-
-    def hop(k):
+        ln = lanes(i, 256)
+        return S.rcopy(hsend.at[k, :, ln], relay.at[k, :, ln], hs.at[k, i], hr.at[k, i],
+                       S.dev(x, rem(y + k2, SIDE), c))
+
+    def hop(k, i):
         k2 = 2 if k else -2
+        ln = lanes(i, 256)
         origin = S.dev(x, rem(y - k2, SIDE), c)["rows"]
         to = rem(origin + (FRAMES if k else total - FRAMES), total)
         has = origin < total - FRAMES if k else origin >= FRAMES
-        return S.rcopy(relay.at[k], hrecv.at[k], vs.at[k], vr.at[k], {"rows": to}), has
+        return S.rcopy(relay.at[k, :, ln], hrecv.at[k, :, ln], vs.at[k, i], vr.at[k, i], {"rows": to}), has
 
     def sends(k):
         return r < total - FRAMES if k else r >= FRAMES
 
-    def halo_start():
+    def halo_start(i):
         for k in (0, 1):
-            pl.when(sends(k))(lambda: halo(k).start())
-
-    def halo_relay():
+            pl.when(sends(k))(lambda: halo(k, i).start())
+
+    def halo_relay(i):
         for k in (0, 1):
-            cp, has = hop(k)
+            cp, has = hop(k, i)
 
             @pl.when(has)
             def _():
-                halo(k).wait_recv()
+                halo(k, i).wait_recv()
                 cp.start()
 
     def halo_finish():
@@ -361,12 +397,22 @@
 
             @pl.when(sends(1 - k))
             def _():
-                hop(k)[0].wait_recv()
+                @pl.loop(0, 5)
+                def _(i):
+                    hop(k, i)[0].wait_recv()
                 vpad[row] = hrecv[k].astype(F32)
 
             @pl.when(jnp.logical_not(sends(1 - k)))
             def _():
                 vpad[row] = jnp.zeros((width, HD), F32)
+
+    def halo_drain():
+        @pl.loop(0, 5)
+        def _(i):
+            for k in (0, 1):
+                pl.when(sends(k))(lambda: halo(k, i).wait_send())
+                cp, has = hop(k, i)
+                pl.when(has)(lambda: cp.wait_send())
 
     def conv_group(g):
         ln = lanes(g, 128)
@@ -389,16 +435,16 @@
         return S.rcopy(pay.at[1 - c], ara, aas, aar, S.dev(x, y, 1 - c))
 
     def ar_x(m):
-        xx = rem(x + m, SIDE)
-        return S.rcopy(red.at[xx], rsx.at[x], xs.at[xx], xr.at[x], S.dev(xx, y, c)), xx
+        k = rem(a + m, SIDE)
+        return S.rcopy(red.at[k], rsx.at[a], xs.at[k], xr.at[a], S.at_ring(k, b))
 
     def ar_y(m):
-        yy = rem(y + m, SIDE)
-        return S.rcopy(part, agy.at[y], ys.at[yy], yr.at[y], S.dev(x, yy, c)), yy
+        k = rem(b + m, SIDE)
+        return S.rcopy(part, agy.at[b], ys.at[k], yr.at[b], S.at_ring(a, k))
 
     def ar_z(m):
-        xx = rem(x + m, SIDE)
-        return S.rcopy(tot, fin.at[c, x], zs.at[xx], zr.at[x], S.dev(xx, y, c)), xx
+        k = rem(a + m, SIDE)
+        return S.rcopy(tot, fin.at[c, a], zs.at[k], zr.at[a], S.at_ring(k, b))
 
     def arrived(m, buf, sem, me):
         k = rem(me + m, SIDE)
@@ -418,48 +464,45 @@
         mine = pay[c] + ara[...]
         for k in range(SIDE):
             red[k] = mine[24 * k:24 * k + 24]
-        rsx[x] = red[x]
+        rsx[a] = red[a]
         for m in range(1, SIDE):
-            ar_x(m)[0].start()
+            ar_x(m).start()
 
     def ar_c():
         for m in range(1, SIDE):
-            arrived(m, rsx, xr, x)
+            arrived(m, rsx, xr, a)
         res = sum8(rsx)
         part[...] = res
-        agy[y] = res
+        agy[b] = res
         for m in range(1, SIDE):
-            ar_y(m)[0].start()
+            ar_y(m).start()
 
     def ar_d():
         for m in range(1, SIDE):
-            arrived(m, agy, yr, y)
+            arrived(m, agy, yr, b)
         res = sum8(agy)
         tot[...] = res
-        fin[c, x] = res
+        fin[c, a] = res
         for m in range(1, SIDE):
-            ar_z(m)[0].start()
+            ar_z(m).start()
 
     def fin_copy(h):
         return S.rcopy(fin.at[h], fin.at[h], es, er, S.dev(x, y, 1 - c))
 
     def ar_e():
         for m in range(1, SIDE):
-            k = rem(x + m, SIDE)
+            k = rem(a + m, SIDE)
             pltpu.make_async_copy(tot, tot, zr.at[k]).wait()
         fin_copy(c).start()
 
     def ar_drain():
         arm().wait_send()
         for m in range(1, SIDE):
-            ar_x(m)[0].wait_send()
-            ar_y(m)[0].wait_send()
-            ar_z(m)[0].wait_send()
+            ar_x(m).wait_send()
+            ar_y(m).wait_send()
+            ar_z(m).wait_send()
         fin_copy(c).wait_send()
-        for k in (0, 1):
-            pl.when(sends(k))(lambda: halo(k).wait_send())
-            cp, has = hop(k)
-            pl.when(has)(lambda: cp.wait_send())
+        halo_drain()
 
     def state_of(g):
         half, gg = g // 5, g % 5
@@ -540,11 +583,15 @@
 
         @pl.when(jnp.logical_and(valid, e == 7))
         def _():
-            S.sib_start(0, rem(b - dl, SIDE))
-
-            @pl.when(dl > 0)
-            def _():
-                S.sib_start(0, rem(b + dl, SIDE))
+            @pl.when(dl == 0)
+            def _():
+                S.sib_start(0, b)
+
+        @pl.when(jnp.logical_and(lax.rem(u, 8) == 7, diag >= 6))
+        def _():
+            for d in (SIDE + 5 - diag, diag - 5):
+                S.paired0(d)
+                S.sib_start(0, rem(b + d, SIDE))
 
         @pl.when(u == 1)
         def _():
@@ -572,9 +619,11 @@
         S.ring2q(0, 0, e, False)
         S.ring2_last(0, e)
         S.ring2_last(0, e + 4)
-    S.sib_start(0, rem(b + 4, SIDE))
     S.sib_start(1, b)
     S.sib_start(2, b)
+    for d in (5, 3, 4):
+        S.paired0(d)
+        S.sib_start(0, rem(b + d, SIDE))
     S.sib_wait(0)
 
     @pl.loop(0, 24)
@@ -588,29 +637,42 @@
                 S.ring2q(1, 0, k, False)
         S.ring2q(typ, dl, e, True)
 
+        @pl.when(jnp.logical_and(u >= 12, u < 16))
+        def _():
+            S.ring2q_last(0, e)
+
         for ty in (0, 1):
-            @pl.when(jnp.logical_and(e == 3, typ == ty))
-            def _():
-                S.sib_start(1 + ty, rem(b - dl, SIDE))
-                S.sib_start(1 + ty, rem(b + dl, SIDE))
-
-        @pl.when(jnp.logical_and(u >= 12, u < 16))
-        def _():
-            S.ring2q_last(0, e)
-
-        @pl.when(u == 15)
-        def _():
+            group = u // 4 - 2
+            d_of = 1 + lax.rem(rem(group, 6), 3)
+
+            @pl.when(jnp.logical_and(jnp.logical_and(e == 1, group >= 0), (group >= 3) == (ty == 1)))
+            def _():
+                for d in (SIDE - d_of, d_of):
+                    S.paired(ty, d)
+                    S.sib_start(1 + ty, rem(b + d, SIDE))
+
+        @pl.when(u == 18)
+        def _():
+            S.paired(0, 4)
             S.sib_start(1, rem(b + 4, SIDE))
 
         @pl.when(u < 5)
         def _():
             value_chunk(u)
 
-        pl.when(u == 4)(halo_start)
+        uh = u - 6 * c
+
+        @pl.when(jnp.logical_and(uh >= 0, uh < 5))
+        def _():
+            halo_start(uh)
 
         @pl.when(jnp.logical_and(u >= 5, u < 10))
         def _():
             key_chunk(u - 5)
+
+        @pl.when(jnp.logical_and(jnp.logical_and(uh >= 7, uh < 17), lax.rem(uh, 2) == 1))
+        def _():
+            halo_relay((uh - 7) // 2)
 
         @pl.when(jnp.logical_and(u >= 10, u < 12))
         def _():
@@ -618,12 +680,11 @@
             def _(k):
                 state_group(5 * (u - 10) + k)
 
-        pl.when(u == 10)(halo_relay)
         pl.when(u == 11)(ar_a)
-        pl.when(u == 12)(ar_b)
-        pl.when(u == 15)(ar_c)
-        pl.when(u == 18)(ar_d)
-        pl.when(u == 17)(drain_first)
+        pl.when(u == 13)(ar_b)
+        pl.when(u == 18)(ar_c)
+        pl.when(u == 23)(ar_d)
+        pl.when(u == 16)(drain_first)
 
         @pl.when(u == 19)
         def _():
@@ -633,18 +694,18 @@
         def _():
             q_chunk(u - 19)
 
-        pl.when(u == 21)(ar_e)
-
+    @pl.loop(0, 4)
+    def _(e):
+        S.ring2q_last(1, e)
+    for d in (6, 2, 5, 3, 4):
+        S.paired(1, d)
+        S.sib_start(2, rem(b + d, SIDE))
+    ar_e()
     halo_finish()
 
     @pl.loop(0, 10)
     def _(g):
         conv_group(g)
-
-    @pl.loop(0, 4)
-    def _(e):
-        S.ring2q_last(1, e)
-    S.sib_start(2, rem(b + 4, SIDE))
     fin_copy(1 - c).wait_recv()
     for g in range(HD // 128):
         linear_group(g)
@@ -675,14 +736,14 @@
             vm((SIDE, 4, UNIT, KP), BF16), vm((2, SIDE // 2, 2, 2, UNIT, KP), BF16),
             vm((4, 20, WIDTHS[0][0]), BF16), vm((8, 10, WMAX), BF16), vm((UNIT, WMAX), F32),
             dma((4,)), dma((4,)), dma((8,)), dma((8,)),
-            dma((2, 2, 8)), dma((2, 8)), dma((2, 2, 4, 8)), dma((2, 8, 8)), dma((3, 8)), dma((3, 8)),
+            dma((2, 7)), dma((2, 8)), dma((2, 2, 4, 8)), dma((2, 8, 8)), dma((3, 8)), dma((3, 8)), dma((2, 7, 8)),
             vm((n, KP), BF16), vm((n, HD), BF16), vm((n, HD), BF16), vm((band + 2, width, HD), F32),
             vm((n, HD), F32), vm((n, HD), BF16), vm((2, width, HD), BF16), vm((2, width, HD), BF16), vm((2, width, HD), BF16),
             vm((2, 192, 128), F32), vm((192, 128), F32), vm((SIDE, 24, 128), F32), vm((SIDE, 24, 128), F32),
             vm((24, 128), F32), vm((SIDE, 24, 128), F32), vm((24, 128), F32), vm((2, SIDE, 24, 128), F32),
-            dma((2,)), dma((2,)), dma((2,)), dma((2,)), dma, dma, dma((8,)), dma((8,)), dma((8,)), dma((8,)), dma((8,)), dma((8,)), dma, dma,
+            dma((2, 5)), dma((2, 5)), dma((2, 5)), dma((2, 5)), dma, dma, dma((8,)), dma((8,)), dma((8,)), dma((8,)), dma((8,)), dma((8,)), dma, dma,
         ],
-        compiler_params=pltpu.CompilerParams(collective_id=0, has_side_effects=True, vmem_limit_bytes=62 << 20),
+        compiler_params=pltpu.CompilerParams(collective_id=0, has_side_effects=True, vmem_limit_bytes=50 << 20),
     )(
         tokens.reshape(n, model), shift, scale, gate, depth_taps,
         pair_weight.T, query_weight.T, output_weight,

time: 162 us -> 153 us (0.944)
  Pallas kernels: 156 us -> 144 us
  local copies, waits for them, and re-layouts: 5.35 us -> 8.2 us
    pallas_call x1, Pallas kernels: 156 us -> 144 us  [body(): pl.pallas_call(kernel, out_shape=(jax.ShapeDtypeStruct((n, model), BF16),...]
    unnamed x2 -> x16, local copies, waits for them, and re-layouts: 5.35 us -> 8.2 us
where the time goes in v3:
time: 153 us
  Pallas kernels  144 us (94%)
  local copies, waits for them, and re-layouts  8.2 us (5%)
    pallas_call x1, Pallas kernels, body(): pl.pallas_call(kernel, out_shape=(jax.ShapeDtypeStruct((n, model), BF16),...  144 us
    unnamed x16, local copies, waits for them, and re-layouts  8.2 us

profile of v3, /device:TPU:513, one launch (start us, length us, event | category | flops | bytes accessed | tf_op | source)
XLA Modules:
  0.0 152.8 jit_solution(7956522873471826244)
XLA Ops:
  0.6 0.0 copy-start
  0.6 0.9 copy-done
  1.5 0.0 copy-start.1
  1.5 0.9 copy-done.1
  2.4 0.0 copy-start.2
  2.4 0.9 copy-done.2
  3.3 0.0 copy-start.3
  3.3 0.9 copy-done.3
  4.2 0.0 copy-start.4
  4.2 0.7 copy-done.4
  4.9 0.0 copy-start.5
  4.9 0.7 copy-done.5
  5.6 0.0 copy-start.6
  5.6 0.7 copy-done.6
  6.3 143.9 %shard_map.95 = (bf16[480,2240]{1,0:T(8,128)(2,1)S(1)}, f32[40,32,32]{2,1,0:T(8,128)S(1)}) custom-call(bf16[480,2240]{1,0:T(8,128)(2,1)} %bitcast.7, f32[2240]{0:T(1024)S(1)} %copy-done.4, f32[2240]{0:T(1024)S(1)} %copy-done.5, f32[2240]{0:T(1024)S(1)} %copy-done.6, f32[9,1280]{1,0:T(8,128)S(1)} %copy-done.1, bf16[20,2240]{1,0:T(8,128)(2,1)S(1)} %bitcast.5, ...), custom_call_target="tpu_custom_call" | custom-call | tf_op jit(solution)/shard_map/pallas_call | solution.py:729
  150.2 1.2 copy.10
  151.4 1.4 copy.12
Async XLA Ops:
  0.6 0.9 copy-start
  1.5 0.9 copy-start.1
  2.4 0.9 copy-start.2
  3.3 0.9 copy-start.3
  4.2 0.7 copy-start.4
  4.9 0.7 copy-start.5
  5.6 0.7 copy-start.6

commit v4 on v3

--- a/solution.py
+++ b/solution.py
@@ -173,8 +173,8 @@
 
     def by_pair(s, typ, e, plane):
         if s == 0:
-            return lax.rem(e, 4) == 1 + plane
-        return e == 1 + lax.rem(typ + plane, 2)
+            return lax.rem(e, 4) == plane
+        return e == lax.rem(typ + plane, 2)
 
     def onward(s, typ, dl, e, dr):
         low = e < (4 if s == 0 else 2)
@@ -225,14 +225,14 @@
 
     def paired(typ, d):
         bb = rem(b + d, SIDE)
-        e = 1 + lax.rem(typ + zp, 2)
+        e = lax.rem(typ + zp, 2)
         aa = pick(1, typ, e, bb)
         by_core(lambda cc: cp2(cc, 1, 0, bb, aa, 3, 4 * typ + e).wait_recv())
 
     def paired0(d):
         bb = rem(b + d, SIDE)
         for k in (0, 4):
-            e = k + 1 + zp
+            e = k + zp
             aa = pick(0, 0, e, bb)
             by_core(lambda cc: cp2(cc, 0, 0, bb, aa, 3, e).wait_recv())
 
@@ -258,14 +258,11 @@
                 def _():
                     by_core(lambda cc: cp2(cc, s, dr, b, a, dl, e8).wait_send())
 
-        @pl.loop(0, 56)
+        @pl.loop(0, 14)
         def _(t):
-            k, e8 = t // 8, lax.rem(t, 8)
-            e, typ = (e8, 0) if s == 0 else (lax.rem(e8, 4), e8 // 4)
-
-            @pl.when(by_pair(s, typ, e, 1 - zp))
-            def _():
-                by_core(lambda cc: zcopy(cc, s, a, b, k, e8).wait_send())
+            k, h = t // 2, lax.rem(t, 2)
+            e8 = 4 * h + (1 - zp if s == 0 else lax.rem(h + 1 - zp, 2))
+            by_core(lambda cc: zcopy(cc, s, a, b, k, e8).wait_send())
 
     def sib_ref(cc, s, bb):
         w = min(s, 1)
@@ -593,32 +590,30 @@
                 S.paired0(d)
                 S.sib_start(0, rem(b + d, SIDE))
 
-        @pl.when(u == 1)
-        def _():
-            norm(20, 24)
-
-        @pl.when(u == 9)
-        def _():
-            norm(24, 30)
+        @pl.when(u == 7)
+        def _():
+            norm(20, 30)
 
         @pl.when(u == 17)
         def _():
             S.phase0_wait(8, 1, st_qo, q0r)
             S.build(1, 8, st_qo)
-
-        step = diag - 3
+            S.ring1(1, jnp.int32(0))
+
         for m2 in (0, 1):
-            e2, ok = level(step, jnp.int32(m2))
-
-            @pl.when(jnp.logical_and(ok, lax.rem(u, 8) == 0))
+            e2, ok = level(diag - 3, jnp.int32(m2))
+
+            @pl.when(jnp.logical_and(jnp.logical_and(ok, diag > 3), lax.rem(u, 8) == 7))
             def _():
                 S.ring1(1, e2)
 
     @pl.loop(0, 4)
     def _(e):
         S.ring2q(0, 0, e, False)
+
+    @pl.loop(0, 8)
+    def _(e):
         S.ring2_last(0, e)
-        S.ring2_last(0, e + 4)
     S.sib_start(1, b)
     S.sib_start(2, b)
     for d in (5, 3, 4):
@@ -697,15 +692,15 @@
     @pl.loop(0, 4)
     def _(e):
         S.ring2q_last(1, e)
+    ar_e()
+    halo_finish()
+
+    @pl.loop(0, 10)
+    def _(g):
+        conv_group(g)
     for d in (6, 2, 5, 3, 4):
         S.paired(1, d)
         S.sib_start(2, rem(b + d, SIDE))
-    ar_e()
-    halo_finish()
-
-    @pl.loop(0, 10)
-    def _(g):
-        conv_group(g)
     fin_copy(1 - c).wait_recv()
     for g in range(HD // 128):
         linear_group(g)
@@ -734,7 +729,7 @@
         scratch_shapes=[
             vm((3, model), F32), vm((20, KP), BF16), vm((2, 10, KP), BF16),
             vm((SIDE, 4, UNIT, KP), BF16), vm((2, SIDE // 2, 2, 2, UNIT, KP), BF16),
-            vm((4, 20, WIDTHS[0][0]), BF16), vm((8, 10, WMAX), BF16), vm((UNIT, WMAX), F32),
+            vm((4, 20, max(WIDTHS[0])), BF16), vm((8, 10, WMAX), BF16), vm((UNIT, WMAX), F32),
             dma((4,)), dma((4,)), dma((8,)), dma((8,)),
             dma((2, 7)), dma((2, 8)), dma((2, 2, 4, 8)), dma((2, 8, 8)), dma((3, 8)), dma((3, 8)), dma((2, 7, 8)),
             vm((n, KP), BF16), vm((n, HD), BF16), vm((n, HD), BF16), vm((band + 2, width, HD), F32),

time: 153 us -> 153 us (level)
  no operation moved by 1% of the time
where the time goes in v4:
time: 153 us
  Pallas kernels  144 us (94%)
  local copies, waits for them, and re-layouts  8.2 us (5%)
    pallas_call x1, Pallas kernels, body(): pl.pallas_call(kernel, out_shape=(jax.ShapeDtypeStruct((n, model), BF16),...  144 us
    unnamed x16, local copies, waits for them, and re-layouts  8.2 us

profile of v4, /device:TPU:513, one launch (start us, length us, event | category | flops | bytes accessed | tf_op | source)
XLA Modules:
  0.0 152.6 jit_solution(2038764613105819142)
XLA Ops:
  0.6 0.0 copy-start
  0.6 0.9 copy-done
  1.5 0.0 copy-start.1
  1.5 0.9 copy-done.1
  2.4 0.0 copy-start.2
  2.4 0.9 copy-done.2
  3.3 0.0 copy-start.3
  3.3 0.9 copy-done.3
  4.2 0.0 copy-start.4
  4.2 0.7 copy-done.4
  4.9 0.0 copy-start.5
  4.9 0.7 copy-done.5
  5.6 0.0 copy-start.6
  5.6 0.7 copy-done.6
  6.3 143.7 %shard_map.95 = (bf16[480,2240]{1,0:T(8,128)(2,1)S(1)}, f32[40,32,32]{2,1,0:T(8,128)S(1)}) custom-call(bf16[480,2240]{1,0:T(8,128)(2,1)} %bitcast.7, f32[2240]{0:T(1024)S(1)} %copy-done.4, f32[2240]{0:T(1024)S(1)} %copy-done.5, f32[2240]{0:T(1024)S(1)} %copy-done.6, f32[9,1280]{1,0:T(8,128)S(1)} %copy-done.1, bf16[20,2240]{1,0:T(8,128)(2,1)S(1)} %bitcast.5, ...), custom_call_target="tpu_custom_call" | custom-call | tf_op jit(solution)/shard_map/pallas_call | solution.py:724
  150.0 1.2 copy.10
  151.2 1.4 copy.12
Async XLA Ops:
  0.6 0.9 copy-start
  1.5 0.9 copy-start.1
  2.4 0.9 copy-start.2
  3.3 0.9 copy-start.3
  4.2 0.7 copy-start.4
  4.9 0.7 copy-start.5
  5.6 0.7 copy-start.6

commit v5 on v4

--- a/solution.py
+++ b/solution.py
@@ -564,48 +564,55 @@
     S.phase0_wait(4, 0, st_kv, p0r)
     S.build(0, 4, st_kv)
 
-    @pl.loop(0, 64)
-    def _(u):
-        diag, dl, m = u // 8, 3 - lax.rem(u // 2, 4), lax.rem(u, 2)
-        e, valid = level(diag - dl, m)
-
-        @pl.when(jnp.logical_and(valid, dl == 0))
-        def _():
-            S.ring1(0, e)
-            S.ring2(0, 0, e, False)
-
-        @pl.when(jnp.logical_and(valid, dl > 0))
-        def _():
-            S.ring2(0, dl, e, True)
-
-        @pl.when(jnp.logical_and(valid, e == 7))
-        def _():
-            @pl.when(dl == 0)
-            def _():
-                S.sib_start(0, b)
-
-        @pl.when(jnp.logical_and(lax.rem(u, 8) == 7, diag >= 6))
-        def _():
-            for d in (SIDE + 5 - diag, diag - 5):
-                S.paired0(d)
-                S.sib_start(0, rem(b + d, SIDE))
-
-        @pl.when(u == 7)
+    @pl.loop(0, 6)
+    def _(diag):
+        low, high = jnp.maximum(diag - 2, 0), jnp.minimum(diag, 3)
+
+        @pl.loop(0, high - low + 1)
+        def _(i):
+            dl = high - i
+            k = diag - dl
+            first = jnp.where(k == 0, 0, jnp.where(k == 1, 1, 5))
+
+            @pl.loop(0, jnp.where(k == 0, 1, jnp.where(k == 1, 4, 3)))
+            def _(m):
+                e = first + m
+
+                @pl.when(dl == 0)
+                def _():
+                    S.ring1(0, e)
+                    S.ring2(0, 0, e, False)
+
+                @pl.when(dl > 0)
+                def _():
+                    S.ring2(0, dl, e, True)
+
+        @pl.when(diag == 0)
         def _():
             norm(20, 30)
 
-        @pl.when(u == 17)
+        @pl.when(diag == 1)
         def _():
             S.phase0_wait(8, 1, st_qo, q0r)
             S.build(1, 8, st_qo)
             S.ring1(1, jnp.int32(0))
 
-        for m2 in (0, 1):
-            e2, ok = level(diag - 3, jnp.int32(m2))
-
-            @pl.when(jnp.logical_and(jnp.logical_and(ok, diag > 3), lax.rem(u, 8) == 7))
-            def _():
-                S.ring1(1, e2)
+        @pl.when(diag == 2)
+        def _():
+            S.sib_start(0, b)
+
+        @pl.when(diag >= 3)
+        def _():
+            S.ring1(1, 2 * diag - 5)
+            S.ring1(1, 2 * diag - 4)
+
+        @pl.when(diag >= 4)
+        def _():
+            for d in (SIDE + 3 - diag, diag - 3):
+                S.paired0(d)
+                S.sib_start(0, rem(b + d, SIDE))
+
+    S.ring1(1, jnp.int32(7))
 
     @pl.loop(0, 4)
     def _(e):
@@ -625,7 +632,7 @@
     def _(u):
         typ, dl, e = u // 12, 1 + lax.rem(u // 4, 3), lax.rem(u, 4)
 
-        @pl.when(u == 12)
+        @pl.when(u == 8 - 3 * c)
         def _():
             @pl.loop(0, 4)
             def _(k):

time: 153 us -> 150 us (0.980)
  Pallas kernels: 144 us -> 140 us
    pallas_call x1, Pallas kernels: 144 us -> 140 us  [body(): pl.pallas_call(kernel, out_shape=(jax.ShapeDtypeStruct((n, model), BF16),...]
where the time goes in v5:
time: 150 us; the launch traced here: 149 us
  Pallas kernels  140 us (93%)
  local copies, waits for them, and re-layouts  8.2 us (5%)
    pallas_call x1, Pallas kernels, body(): pl.pallas_call(kernel, out_shape=(jax.ShapeDtypeStruct((n, model), BF16),...  140 us
    unnamed x16, local copies, waits for them, and re-layouts  8.2 us

profile of v5, /device:TPU:513, one launch (start us, length us, event | category | flops | bytes accessed | tf_op | source)
XLA Modules:
  0.0 149.2 jit_solution(726670003341945037)
XLA Ops:
  0.6 0.0 copy-start
  0.6 0.9 copy-done
  1.5 0.0 copy-start.1
  1.5 0.9 copy-done.1
  2.4 0.0 copy-start.2
  2.4 0.9 copy-done.2
  3.3 0.0 copy-start.3
  3.3 0.9 copy-done.3
  4.2 0.0 copy-start.4
  4.2 0.7 copy-done.4
  4.9 0.0 copy-start.5
  4.9 0.7 copy-done.5
  5.6 0.0 copy-start.6
  5.6 0.7 copy-done.6
  6.3 140.3 %shard_map.95 = (bf16[480,2240]{1,0:T(8,128)(2,1)S(1)}, f32[40,32,32]{2,1,0:T(8,128)S(1)}) custom-call(bf16[480,2240]{1,0:T(8,128)(2,1)} %bitcast.7, f32[2240]{0:T(1024)S(1)} %copy-done.4, f32[2240]{0:T(1024)S(1)} %copy-done.5, f32[2240]{0:T(1024)S(1)} %copy-done.6, f32[9,1280]{1,0:T(8,128)S(1)} %copy-done.1, bf16[20,2240]{1,0:T(8,128)(2,1)S(1)} %bitcast.5, ...), custom_call_target="tpu_custom_call" | custom-call | tf_op jit(solution)/shard_map/pallas_call | solution.py:731
  146.6 1.2 copy.10
  147.8 1.4 copy.12
Async XLA Ops:
  0.6 0.9 copy-start
  1.5 0.9 copy-start.1
  2.4 0.9 copy-start.2
  3.3 0.9 copy-start.3
  4.2 0.7 copy-start.4
  4.9 0.7 copy-start.5
  5.6 0.7 copy-start.6

commit v6 on v5

--- a/solution.py
+++ b/solution.py
@@ -545,6 +545,13 @@
         S.ring1_drain(1)
         S.ring2_drain(0)
         S.sib_drain(0)
+
+    def convolve():
+        halo_finish()
+
+        @pl.loop(0, HD // 128)
+        def _(g):
+            conv_group(g)
 
     mod[0, :] = shift[...]
     mod[1, :] = scale[...]
@@ -696,30 +703,28 @@
         def _():
             q_chunk(u - 19)
 
+        pl.when(jnp.logical_and(u == 21, c == 0))(convolve)
+
     @pl.loop(0, 4)
     def _(e):
         S.ring2q_last(1, e)
     ar_e()
-    halo_finish()
-
-    @pl.loop(0, 10)
-    def _(g):
-        conv_group(g)
+    pl.when(c == 1)(convolve)
     for d in (6, 2, 5, 3, 4):
         S.paired(1, d)
         S.sib_start(2, rem(b + d, SIDE))
     fin_copy(1 - c).wait_recv()
     for g in range(HD // 128):
         linear_group(g)
+    ar_drain()
+    S.ring2_drain(1)
+    S.sib_drain(1)
     S.sib_wait(2)
 
     @pl.loop(0, 8)
     def _(i):
         out_chunk(pl.multiple_of(i * 256, 256), 256)
     out_chunk(2048, 192)
-    ar_drain()
-    S.ring2_drain(1)
-    S.sib_drain(1)
     S.sib_drain(2)
 
 

time: 150 us -> 148 us (0.987)
  Pallas kernels: 140 us -> 138 us
    pallas_call x1, Pallas kernels: 140 us -> 138 us  [body(): pl.pallas_call(kernel, out_shape=(jax.ShapeDtypeStruct((n, model), BF16),...]
where the time goes in v6:
time: 148 us; the launch traced here: 147 us
  Pallas kernels  138 us (93%)
  local copies, waits for them, and re-layouts  8.2 us (6%)
    pallas_call x1, Pallas kernels, body(): pl.pallas_call(kernel, out_shape=(jax.ShapeDtypeStruct((n, model), BF16),...  138 us
    unnamed x16, local copies, waits for them, and re-layouts  8.2 us

profile of v6, /device:TPU:513, one launch (start us, length us, event | category | flops | bytes accessed | tf_op | source)
XLA Modules:
  0.0 147.3 jit_solution(3031016951469792921)
XLA Ops:
  0.6 0.0 copy-start
  0.6 0.9 copy-done
  1.5 0.0 copy-start.1
  1.5 0.9 copy-done.1
  2.4 0.0 copy-start.2
  2.4 0.9 copy-done.2
  3.3 0.0 copy-start.3
  3.3 0.9 copy-done.3
  4.2 0.0 copy-start.4
  4.2 0.7 copy-done.4
  4.9 0.0 copy-start.5
  4.9 0.7 copy-done.5
  5.6 0.0 copy-start.6
  5.6 0.7 copy-done.6
  6.3 138.4 %shard_map.95 = (bf16[480,2240]{1,0:T(8,128)(2,1)S(1)}, f32[40,32,32]{2,1,0:T(8,128)S(1)}) custom-call(bf16[480,2240]{1,0:T(8,128)(2,1)} %bitcast.7, f32[2240]{0:T(1024)S(1)} %copy-done.4, f32[2240]{0:T(1024)S(1)} %copy-done.5, f32[2240]{0:T(1024)S(1)} %copy-done.6, f32[9,1280]{1,0:T(8,128)S(1)} %copy-done.1, bf16[20,2240]{1,0:T(8,128)(2,1)S(1)} %bitcast.5, ...), custom_call_target="tpu_custom_call" | custom-call | tf_op jit(solution)/shard_map/pallas_call | solution.py:736
  144.7 1.2 copy.10
  145.9 1.4 copy.12
Async XLA Ops:
  0.6 0.9 copy-start
  1.5 0.9 copy-start.1
  2.4 0.9 copy-start.2
  3.3 0.9 copy-start.3
  4.2 0.7 copy-start.4
  4.9 0.7 copy-start.5
  5.6 0.7 copy-start.6
